TPU v7x, 128 devices: a whole 4x4x4 slice. The times are simulated.
128 devices in a mesh: group: 8 (over y_hi, z), shard: 16 (over x, y_lo, core).
Axes of the slice: x: 4, y: 4 (y_hi: 2, y_lo: 2; y = y_hi * 2 + y_lo), z: 4, core: 2. Of those that a mesh axis runs over, the one named last changes fastest.
Arguments:
- hidden_state: bfloat16 [2048, 8192], P('group', 'shard'), may hold values from -40 to 40
- attn_gain: bfloat16 [8192], replicated, may hold values from 0.5 to 1.5
- ffn_gain: bfloat16 [8192], replicated, may hold values from 0.5 to 1.5
- w_query: bfloat16 [8192, 8192], P('group', 'shard'), may hold values from -0.125 to 0.125
- w_keyval: bfloat16 [8192, 2048], P('group', 'shard'), may hold values from -0.0625 to 0.0625
- w_output: bfloat16 [8192, 8192], P('shard', 'group'), may hold values from -0.0625 to 0.0625
- cache_keys: bfloat16 [2048, 8, 192, 128], P(('group', 'shard')), may hold values from -256 to 256
- cache_values: bfloat16 [2048, 8, 192, 128], P(('group', 'shard')), may hold values from -6 to 6
- lengths: int32 [2048], P('group'), may hold values from 2 to 192, as said below
Outputs:
- branch: bfloat16 [2048, 8192], P('group', 'shard')
- ffn_input: bfloat16 [2048, 8192], P('group', 'shard')
Inputs may be any that keep to these rules, and one draw needn't show every extreme that they name: `lengths`: in every aligned block of 16 sequences, at least one has all 192 cached positions live.
All inputs are finite; a program needn't handle non-finite values.
Results may differ from a plain program's by a relative error of at most 0.012.
The roundings to bfloat16 on the way count: a program that leaves them out, or rounds other values in their place, can miss the bound.
Values may be sent and summed in bfloat16 or wider, within the bound.
No kernel may reach another device: no remote copies, remote signals or barrier semaphores. Data moves between devices by JAX's collectives and lax.ppermute only.
A program may use at most 128 MiB of HBM per device.

v0:
```python
import jax
import jax.numpy as jnp
from jax import lax
from jax.experimental import pallas as pl
from jax.experimental.pallas import tpu as pltpu
from jax.sharding import Mesh, PartitionSpec as P

EPS = 1e-05
ROPE_BASE = 500000.0
F32 = jnp.float32
BF16 = jnp.bfloat16


PAIR = ("yl", "c")
WIDE = ("yh", "zh", "x")


def rotate(v, position):
    half = v.shape[-1] // 2
    freq = ROPE_BASE ** (-2.0 * jnp.arange(half, dtype=F32) / v.shape[-1])
    angles = position.astype(F32)[:, None] * freq[None, :]
    cos = jnp.cos(angles)[:, None, :]
    sin = jnp.sin(angles)[:, None, :]
    low, high = v[..., :half], v[..., half:]
    return jnp.concatenate([low * cos - high * sin, high * cos + low * sin], axis=-1)


def attend(grouped, new_keys, new_values, cache_keys, cache_values, lengths):
    _, _, cache_len, head_dim = cache_keys.shape
    scale = head_dim ** (-0.5)
    scores = jnp.einsum("nkgd,nkld->nkgl", grouped, cache_keys, preferred_element_type=F32) * scale
    self_score = jnp.einsum("nkgd,nkd->nkg", grouped, new_keys, preferred_element_type=F32) * scale
    live = jnp.arange(cache_len, dtype=jnp.int32)[None, :] < lengths[:, None]
    scores = jnp.where(live[:, None, None, :], scores, -1e30)
    top = jnp.maximum(jnp.max(scores, axis=3), self_score)
    e = jnp.exp(scores - top[..., None])
    e_self = jnp.exp(self_score - top)
    denom = jnp.sum(e, axis=3) + e_self
    weights = (e / denom[..., None]).astype(BF16)
    w_self = (e_self / denom).astype(BF16)
    context = jnp.einsum("nkgl,nkld->nkgd", weights, cache_values, preferred_element_type=F32)
    context = context + w_self.astype(F32)[..., None] * new_values.astype(F32)[:, :, None, :]
    return context.astype(BF16)


def xor_pairs(k):
    return [(i, i ^ k) for i in range(4)]


SPREAD = [(g * 4 + x, x * 4 + (g ^ x)) for g in range(4) for x in range(4)]
COLLECT = [(g * 4 + x, (x ^ 1) * 4 + g) for g in range(4) for x in range(4)]
FLIP = [(0, 1), (1, 0)]


def swap(v, axis):
    return lax.ppermute(v, axis, FLIP)


def cube_of(w):
    half = w.shape[0] // 2
    far_z, far_y = swap(w, "zl"), swap(w, "yl")
    top, bottom = swap(far_z[:half], "yl"), swap(far_y[half:], "zl")
    pieces = []
    for dz, dy, row, v in ((0, 0, 0, w), (1, 0, 0, far_z), (0, 1, 0, far_y), (1, 1, 0, top), (1, 1, half, bottom)):
        pieces += [(dz, dy, 0, row, v), (dz, dy, 1, row, swap(v, "c"))]
    return pieces


def matmul_kernel(lhs_pieces, weights, out_shape, place, finish, scalars):
    n = len(weights)

    def body(scalar_ref, *refs):
        lhs_refs, w_refs = refs[: len(lhs_pieces)], refs[len(lhs_pieces) : len(lhs_pieces) + n]
        out_ref, lhs_scr = refs[len(lhs_pieces) + n], refs[len(lhs_pieces) + n + 1]
        bufs, sem = refs[len(lhs_pieces) + n + 2 : -1], refs[-1]
        copies = [pltpu.make_async_copy(w_refs[i], bufs[i], sem.at[i]) for i in range(n)]
        for copy in copies:
            copy.start()
        place(scalar_ref, lhs_refs, lhs_scr)
        slots = sorted({slot for _, slot, _ in weights})
        for slot in slots:
            acc = None
            for i, (col, at, w) in enumerate(weights):
                if at != slot:
                    continue
                copies[i].wait()
                term = jnp.dot(lhs_scr[:, col : col + w.shape[0]], bufs[i][...], preferred_element_type=F32)
                acc = term if acc is None else acc + term
            finish(scalar_ref, out_ref, slot, acc.astype(BF16))

    rows = sum(v.shape[0] for v in lhs_pieces)
    depth = lhs_pieces[0].shape[1]
    flops = sum(2 * rows * w.size for _, _, w in weights)
    return pl.pallas_call(
        body,
        out_shape=jax.ShapeDtypeStruct(out_shape, BF16),
        in_specs=[pl.BlockSpec(memory_space=pltpu.SMEM)]
        + [pl.BlockSpec(memory_space=pltpu.VMEM)] * len(lhs_pieces)
        + [pl.BlockSpec(memory_space=pltpu.HBM)] * n,
        out_specs=pl.BlockSpec(memory_space=pltpu.VMEM),
        scratch_shapes=[pltpu.VMEM((rows, depth), BF16)]
        + [pltpu.VMEM(w.shape, BF16) for _, _, w in weights]
        + [pltpu.SemaphoreType.DMA((n,))],
        compiler_params=pltpu.CompilerParams(vmem_limit_bytes=30 << 20),
        cost_estimate=pl.CostEstimate(flops=flops, bytes_accessed=sum(2 * w.size for _, _, w in weights), transcendentals=0),
    )(jnp.stack(scalars).astype(jnp.int32), *lhs_pieces, *[w for _, _, w in weights])


def unrelated(pieces, index):
    n = len(pieces)
    out = []
    for j in range(n):
        v = pieces[j]
        for k in range(1, n):
            v = jnp.where(index == k, pieces[j ^ k], v)
        out.append(v)
    return out


def sum_over_x(v):
    return sum((lax.ppermute(v, "x", xor_pairs(k)) for k in (1, 2, 3)), v)


def local(h, attn_gain, ffn_gain, w_query, w_keyval, w_output, cache_keys, cache_values, lengths):
    x_pos = lax.axis_index("x")
    shard = lax.axis_index(("x", "yl", "c"))
    seq_dev, kv_heads, _, head_dim = cache_keys.shape
    tokens, width = h.shape
    quarter = tokens // 4
    model = 16 * width
    wide = 4 * width

    q_cols = w_query.shape[1]
    rows, cols = w_query.shape[0], q_cols + w_keyval.shape[1]
    w_qkv = cube_of(jnp.concatenate([w_query, w_keyval], axis=1))
    w_out = cube_of(w_output)

    sent = h.reshape(4, 4, seq_dev, width).transpose(1, 0, 2, 3).reshape(4, quarter, width)
    got = lax.all_to_all(sent, PAIR, 0, 0, tiled=True)
    resident = got.transpose(1, 0, 2).reshape(quarter, wide).astype(F32)
    squares = sum_over_x(jnp.sum(resident * resident, axis=1))
    inverse = lax.rsqrt(squares / model + EPS)[:, None]
    gain = lax.dynamic_slice_in_dim(attn_gain, x_pos * wide, wide).astype(F32)
    normed = (resident * inverse * gain).astype(BF16)
    z_pos = lax.axis_index("zl")
    normed = jnp.concatenate(unrelated([normed[:, :rows], normed[:, rows:]], z_pos), axis=1)
    normed = lax.ppermute(normed, WIDE, SPREAD)
    slots = [normed] + [lax.ppermute(normed, "x", xor_pairs(k)) for k in (1, 2, 3)]

    order = lax.axis_index("x") ^ lax.axis_index(("yh", "zh"))

    def place_tokens(scalar_ref, lhs_refs, lhs_scr):
        for k, ref in enumerate(lhs_refs):
            at = pl.multiple_of((scalar_ref[0] ^ k) * quarter, quarter)
            lhs_scr[pl.ds(at, quarter), :] = ref[...]

    def put_columns(scalar_ref, out_ref, slot, value):
        out_ref[:, slot * cols : (slot + 1) * cols] = value

    partial = matmul_kernel(
        slots,
        [(dz * rows + row, dy * 2 + dc, v) for dz, dy, dc, row, v in w_qkv],
        (tokens, 4 * cols),
        place_tokens,
        put_columns,
        [order],
    ).reshape(16, seq_dev, 4 * cols)
    arrived = lax.all_to_all(partial, WIDE, 0, 0, tiled=True)
    qkv = jnp.sum(arrived.reshape(4, 4, seq_dev, 4 * cols).astype(F32), axis=0)
    pair_pos = lax.axis_index(PAIR)
    q_of = [unrelated([qkv[x, :, p * cols : p * cols + q_cols] for p in range(4)], pair_pos) for x in range(4)]
    kv_of = [unrelated([qkv[x, :, p * cols + q_cols : (p + 1) * cols] for p in range(4)], pair_pos) for x in range(4)]
    queries = jnp.concatenate([v for x in q_of for v in x], axis=1).reshape(seq_dev, -1, head_dim)
    keyval = jnp.concatenate([v for x in kv_of for v in x], axis=1).reshape(seq_dev, -1, head_dim)
    own_len = lax.dynamic_slice_in_dim(lengths, shard * seq_dev, seq_dev)
    roped_q = rotate(queries, own_len).astype(BF16)
    new_keys = rotate(keyval[:, :kv_heads], own_len).astype(BF16)
    new_values = keyval[:, kv_heads:].astype(BF16)
    per_kv = roped_q.shape[1] // kv_heads
    grouped = roped_q.reshape(seq_dev, kv_heads, per_kv, head_dim)
    context = attend(grouped, new_keys, new_values, cache_keys, cache_values, own_len)

    context = context.reshape(seq_dev, 4, wide).transpose(1, 0, 2)
    context = jnp.broadcast_to(context[None], (4, 4, seq_dev, wide)).reshape(16, seq_dev, wide)
    context = lax.all_to_all(context, WIDE, 0, 0, tiled=True).reshape(tokens, wide)

    def place_heads(scalar_ref, lhs_refs, lhs_scr):
        for p in range(4):
            at = pl.multiple_of((scalar_ref[0] ^ p) * width, width)
            lhs_scr[:, p * width : (p + 1) * width] = lhs_refs[0][:, pl.ds(at, width)]

    def put_blocks(scalar_ref, out_ref, slot, value):
        n = value.shape[1]
        at = pl.multiple_of((scalar_ref[1] ^ slot) * n, n)
        for j in range(4):
            out_ref[j ^ 1, :, pl.ds(at, n)] = value[j * quarter : (j + 1) * quarter]

    out = matmul_kernel(
        [context],
        [((dy * 2 + dc) * width + row, dz, v) for dz, dy, dc, row, v in w_out],
        (4, quarter, wide),
        place_heads,
        put_blocks,
        [pair_pos, z_pos],
    )
    out = lax.all_to_all(out, "x", 0, 0, tiled=True)
    out = jnp.sum(out.astype(F32), axis=0).astype(BF16)
    branch = lax.ppermute(out, WIDE, COLLECT)
    stream = resident + branch.astype(F32)
    squares_two = sum_over_x(jnp.sum(stream * stream, axis=1))
    inverse_two = lax.rsqrt(squares_two / model + EPS)[:, None]
    gain_two = lax.dynamic_slice_in_dim(ffn_gain, x_pos * wide, wide).astype(F32)
    ffn_input = (stream * inverse_two * gain_two).astype(BF16)
    both = jnp.stack([branch, ffn_input]).reshape(2, quarter, 4, width).transpose(2, 0, 1, 3)
    both = lax.all_to_all(both, PAIR, 0, 0, tiled=True)
    both = both.reshape(4, 2, 4, seq_dev, width).transpose(1, 2, 0, 3, 4).reshape(2, tokens, width)
    return both[0], both[1]


def solution(mesh):
    fine = Mesh(mesh.devices.reshape(2, 2, 2, 4, 2, 2), ("yh", "zh", "zl", "x", "yl", "c"))
    group = ("yh", "zh", "zl")
    shard = ("x", "yl", "c")
    placed = (
        P(group, shard),
        P(),
        P(),
        P(group, shard),
        P(group, shard),
        P(shard, group),
        P(group + shard, None, None, None),
        P(group + shard, None, None, None),
        P(group),
    )
    return jax.shard_map(
        local,
        mesh=fine,
        in_specs=placed,
        out_specs=(P(group, shard), P(group, shard)),
        check_vma=False,
    )
```

profile of v0, /device:TPU:1, one launch (start us, length us, event | category | flops | bytes accessed | tf_op | source)
XLA Modules:
  0.0 239.1 jit_solution(6125080073485458450)
XLA Ops:
  2.4 4.9 %all-to-all-start = ((bf16[4,64,512]{2,1,0:T(8,128)(2,1)}), bf16[4,64,512]{2,1,0:T(8,128)(2,1)S(1)}, u32[]{:S(2)}, u32[]{:S(2)}) async-start(bf16[4,64,512]{2,1,0:T(8,128)(2,1)} %bitcast.5), calls=%async_computation | async-start | bytes 524288 | tf_op jit(solution)/shard_map/all_to_all | solution.py:139
  13.9 2.5 %collective-permute-start.1 = (f32[64]{0:T(128)S(1)}, f32[64]{0:T(128)S(1)}, u32[]{:S(2)}, u32[]{:S(2)}) collective-permute-start(f32[64]{0:T(128)S(1)} %fusion.3), channel_id=1, source_target_pairs={{0,8},{4,12},{8,0},{12,4},{1,9},{5,13},{9,1},{13,5},{2,10},{6,14},... | collective-permute-start | bytes 776 | tf_op jit(solution)/shard_map/ppermute | solution.py:121
  17.8 2.2 collective-permute-done.2
  20.8 23.3 %collective-permute-start.4 = (bf16[64,2048]{1,0:T(8,128)(2,1)S(1)}, bf16[64,2048]{1,0:T(8,128)(2,1)S(1)}, u32[]{:S(2)}, u32[]{:S(2)}) collective-permute-start(bf16[64,2048]{1,0:T(8,128)(2,1)S(1)} %collective-permute-done.3.refs_0_), channel_id=1, source_target_pairs={{0,4},{4,0},{8,12},{12,8},{1,5},{5,1},{9,13},{13,9},{2,6},{6,2},{1... | collective-permute-start | bytes 786440 | tf_op jit(solution)/shard_map/ppermute | solution.py:148
  44.2 3.2 %collective-permute-start.5 = (bf16[64,2048]{1,0:T(8,128)(2,1)S(1)}, bf16[64,2048]{1,0:T(8,128)(2,1)S(1)}, u32[]{:S(2)}, u32[]{:S(2)}) collective-permute-start(bf16[64,2048]{1,0:T(8,128)(2,1)S(1)} %collective-permute-done.3.refs_0_), channel_id=1, source_target_pairs={{0,8},{4,12},{8,0},{12,4},{1,9},{5,13},{9,1},{13,5},{2,10},{6,14},... | collective-permute-start | bytes 786440 | tf_op jit(solution)/shard_map/ppermute | solution.py:148
  47.4 2.2 collective-permute-start.7
  54.3 3.6 %collective-permute-done.5.refs_2_ = bf16[64,2048]{1,0:T(8,128)(2,1)S(1)} collective-permute-done((bf16[64,2048]{1,0:T(8,128)(2,1)S(1)}, bf16[64,2048]{1,0:T(8,128)(2,1)S(1)}, u32[]{:S(2)}, u32[]{:S(2)}) %collective-permute-start.5) | collective-permute-done | bytes 262176 | tf_op jit(solution)/shard_map/ppermute | solution.py:148
  58.6 2.4 %collective-permute-start.11 = (bf16[1024,640]{1,0:T(8,128)(2,1)}, bf16[1024,640]{1,0:T(8,128)(2,1)}, u32[]{:S(2)}, u32[]{:S(2)}) collective-permute-start(bf16[1024,640]{1,0:T(8,128)(2,1)} %collective-permute-done.10.refs_8_), channel_id=1, source_target_pairs={{0,1},{1,0},{2,3},{3,2},{4,5},{5,4},{6,7},{7,6},{8,9},{9,8},{10,11... | collective-permute-start | bytes 3932168 | tf_op jit(solution)/shard_map/ppermute | solution.py:56
  63.6 2.5 %collective-permute-done.12.refs_10_ = bf16[512,640]{1,0:T(8,128)(2,1)S(1)} collective-permute-done((bf16[512,640]{1,0:T(8,128)(2,1)S(1)}, bf16[512,640]{1,0:T(8,128)(2,1)S(1)}, u32[]{:S(2)}, u32[]{:S(2)}) %collective-permute-start.12) | collective-permute-done | bytes 655392 | tf_op jit(solution)/shard_map/ppermute | solution.py:56
  66.8 2.1 collective-permute-done.14.refs_12_
  70.1 2.1 collective-permute-done.15.refs_13_
  75.1 6.6 %shard_map.104 = bf16[256,2560]{1,0:T(8,128)(2,1)} custom-call(s32[1]{0:T(128)} %bitcast.2.scalar_ref, bf16[64,2048]{1,0:T(8,128)(2,1)S(1)} %collective-permute-done.3.refs_0_, bf16[64,2048]{1,0:T(8,128)(2,1)S(1)} %copy-done.5, bf16[64,2048]{1,0:T(8,128)(2,1)S(1)} %copy-done.7, bf16[64,2048]{1,0:T(8,128)(2,1)S(1)} %copy-done.9, ...), custom_call_target="tpu_custom_call" | custom-call | flops 2684354560 | bytes 10485760 | tf_op jit(solution)/shard_map/pallas_call | solution.py:94
  81.7 11.3 %all-to-all-start.1 = ((bf16[16,16,2560]{2,1,0:T(8,128)(2,1)}), bf16[16,16,2560]{2,1,0:T(8,128)(2,1)S(1)}, u32[]{:S(2)}, u32[]{:S(2)}) async-start(bf16[16,16,2560]{2,1,0:T(8,128)(2,1)} %bitcast.7), calls=%async_computation.1 | async-start | bytes 2621440 | tf_op jit(solution)/shard_map/all_to_all | solution.py:168
  95.1 35.7 %collective-permute-done.17.refs_3_ = bf16[512,1024]{1,0:T(8,128)(2,1)S(1)} collective-permute-done((bf16[512,1024]{1,0:T(8,128)(2,1)}, bf16[512,1024]{1,0:T(8,128)(2,1)S(1)}, u32[]{:S(2)}, u32[]{:S(2)}) %collective-permute-start.17) | collective-permute-done | bytes 1048608 | tf_op jit(solution)/shard_map/ppermute | solution.py:56
  142.0 6.6 %fusion.26 = (f32[16,8,8]{2,1,0:T(8,128)S(1)}, f32[16,8,8,192]{3,2,1,0:T(8,128)S(1)}) fusion(bf16[16,8,192,128]{3,2,1,0:T(8,128)(2,1)} %param.15, bf16[16,8,8,64]{3,2,1,0:T(8,128)(2,1)S(1)} %get-tuple-element.31, bf16[16,8,8,64]{3,2,1,0:T(8,128)(2,1)S(1)} %get-tuple-element.30, pred[16,192]{1,0:T(8,128)(4,1)S(1)} %iota_compare_fusion), kind=kOutput, calls=%fused_computation.117 | convolution fusion | flops 51444736 | bytes 7347200 | tf_op jit(solution)/shard_map/nkgd,nkld->nkgl/dot_general | solution.py:31
  152.3 9.4 %all-to-all-start.2 = ((bf16[16,16,2048]{2,1,0:T(8,128)(2,1)}), bf16[16,16,2048]{2,1,0:T(8,128)(2,1)S(1)}, u32[]{:S(2)}, u32[]{:S(2)}) async-start(bf16[16,16,2048]{2,1,0:T(8,128)(2,1)} %bitcast.170), calls=%async_computation.2 | async-start | bytes 2097152 | tf_op jit(solution)/shard_map/all_to_all | solution.py:185
  166.0 14.7 %all-to-all-done.2 = bf16[16,16,2048]{2,1,0:T(8,128)(2,1)S(1)} async-done(((bf16[16,16,2048]{2,1,0:T(8,128)(2,1)}), bf16[16,16,2048]{2,1,0:T(8,128)(2,1)S(1)}, u32[]{:S(2)}, u32[]{:S(2)}) %all-to-all-start.2) | async-done | bytes 1048608 | tf_op jit(solution)/shard_map/all_to_all | solution.py:185
  182.7 5.1 %shard_map.105 = bf16[4,64,2048]{2,1,0:T(8,128)(2,1)S(1)} custom-call(s32[2]{0:T(128)S(1)} %pad_add_fusion.scalar_ref, bf16[256,2048]{1,0:T(8,128)(2,1)S(1)} %bitcast.165, bf16[512,1024]{1,0:T(8,128)(2,1)} %refs_1_.1, bf16[512,1024]{1,0:T(8,128)(2,1)} %collective-permute-done.16.refs_2_, bf16[512,1024]{1,0:T(8,128)(2,1)S(1)} %collective-permute-done.17.refs_3_, ...), custom_call_target="tpu_custom_call" | custom-call | flops 2147483648 | bytes 8388608 | tf_op jit(solution)/shard_map/pallas_call | solution.py:94
  187.8 15.8 %all_to_all.25 = bf16[4,64,2048]{2,1,0:T(8,128)(2,1)S(1)} all-to-all(bf16[4,64,2048]{2,1,0:T(8,128)(2,1)S(1)} %shard_map.105), channel_id=1, replica_groups=mesh['yh'=2,'zh'=2,'zl'=2,'x'=4,'yl'=2,'c'=2] {'x'}, dimensions={0} | all-to-all | bytes 2097152 | tf_op jit(solution)/shard_map/all_to_all | solution.py:206
  203.9 2.1 collective-permute-start.25
  206.0 3.7 %collective-permute-done.25 = bf16[64,2048]{1,0:T(8,128)(2,1)S(1)} collective-permute-done((bf16[64,2048]{1,0:T(8,128)(2,1)S(1)}, bf16[64,2048]{1,0:T(8,128)(2,1)S(1)}, u32[]{:S(2)}, u32[]{:S(2)}) %collective-permute-start.25) | collective-permute-done | bytes 262176 | tf_op jit(solution)/shard_map/ppermute | solution.py:208
  211.2 9.3 %collective-permute-start.27 = (f32[64]{0:T(128)S(1)}, f32[64]{0:T(128)S(1)}, u32[]{:S(2)}, u32[]{:S(2)}) collective-permute-start(f32[64]{0:T(128)S(1)} %multiply_reduce_fusion), channel_id=1, source_target_pairs={{0,8},{4,12},{8,0},{12,4},{1,9},{5,13},{9,1},{13,5},{2,10},{6,14},... | collective-permute-start | bytes 776 | tf_op jit(solution)/shard_map/ppermute | solution.py:121
  221.5 2.7 %collective-permute-done.28 = f32[64]{0:T(128)S(1)} collective-permute-done((f32[64]{0:T(128)S(1)}, f32[64]{0:T(128)S(1)}, u32[]{:S(2)}, u32[]{:S(2)}) %collective-permute-start.28) | collective-permute-done | bytes 288 | tf_op jit(solution)/shard_map/ppermute | solution.py:121
  224.6 13.1 %all_to_all.26 = bf16[4,2,64,512]{3,2,1,0:T(8,128)(2,1)S(1)} all-to-all(bf16[4,2,64,512]{3,2,1,0:T(8,128)(2,1)S(1)} %maximum_bitcast_fusion), channel_id=1, replica_groups=mesh['yh'=2,'zh'=2,'zl'=2,'x'=4,'yl'=2,'c'=2] {'yl','c'}, dimensions={0} | all-to-all | bytes 1048576 | tf_op jit(solution)/shard_map/all_to_all | solution.py:215
  (159 shorter events, 51.1 us)
Async XLA Ops:
  2.4 9.9 %all-to-all-start = ((bf16[4,64,512]{2,1,0:T(8,128)(2,1)}), bf16[4,64,512]{2,1,0:T(8,128)(2,1)S(1)}, u32[]{:S(2)}, u32[]{:S(2)}) async-start(bf16[4,64,512]{2,1,0:T(8,128)(2,1)} %bitcast.5), calls=%async_computation | async-start | bytes 524288 | tf_op jit(solution)/shard_map/all_to_all | solution.py:139
  7.4 39.9 %collective-permute-start.8 = (bf16[1024,640]{1,0:T(8,128)(2,1)S(1)}, bf16[1024,640]{1,0:T(8,128)(2,1)S(1)}, u32[]{:S(2)}, u32[]{:S(2)}) collective-permute-start(bf16[1024,640]{1,0:T(8,128)(2,1)S(1)} %constant_dynamic-update-slice_fusion.refs_4_), channel_id=1, source_target_pairs={{0,16},{16,0},{1,17},{17,1},{2,18},{18,2},{3,19},{19,3},{4,20},{20... | collective-permute-start | bytes 3932168 | tf_op jit(solution)/shard_map/ppermute | solution.py:56
  9.3 40.3 %collective-permute-start.10 = (bf16[1024,640]{1,0:T(8,128)(2,1)S(1)}, bf16[1024,640]{1,0:T(8,128)(2,1)}, u32[]{:S(2)}, u32[]{:S(2)}) collective-permute-start(bf16[1024,640]{1,0:T(8,128)(2,1)S(1)} %constant_dynamic-update-slice_fusion.refs_4_), channel_id=1, source_target_pairs={{0,2},{2,0},{1,3},{3,1},{4,6},{6,4},{5,7},{7,5},{8,10},{10,8},{9,1... | collective-permute-start | bytes 3932168 | tf_op jit(solution)/shard_map/ppermute | solution.py:56
  20.8 31.1 %collective-permute-start.4 = (bf16[64,2048]{1,0:T(8,128)(2,1)S(1)}, bf16[64,2048]{1,0:T(8,128)(2,1)S(1)}, u32[]{:S(2)}, u32[]{:S(2)}) collective-permute-start(bf16[64,2048]{1,0:T(8,128)(2,1)S(1)} %collective-permute-done.3.refs_0_), channel_id=1, source_target_pairs={{0,4},{4,0},{8,12},{12,8},{1,5},{5,1},{9,13},{13,9},{2,6},{6,2},{1... | collective-permute-start | bytes 786440 | tf_op jit(solution)/shard_map/ppermute | solution.py:148
  44.2 13.7 %collective-permute-start.5 = (bf16[64,2048]{1,0:T(8,128)(2,1)S(1)}, bf16[64,2048]{1,0:T(8,128)(2,1)S(1)}, u32[]{:S(2)}, u32[]{:S(2)}) collective-permute-start(bf16[64,2048]{1,0:T(8,128)(2,1)S(1)} %collective-permute-done.3.refs_0_), channel_id=1, source_target_pairs={{0,8},{4,12},{8,0},{12,4},{1,9},{5,13},{9,1},{13,5},{2,10},{6,14},... | collective-permute-start | bytes 786440 | tf_op jit(solution)/shard_map/ppermute | solution.py:148
  47.4 13.7 %collective-permute-start.6 = (bf16[64,2048]{1,0:T(8,128)(2,1)S(1)}, bf16[64,2048]{1,0:T(8,128)(2,1)S(1)}, u32[]{:S(2)}, u32[]{:S(2)}) collective-permute-start(bf16[64,2048]{1,0:T(8,128)(2,1)S(1)} %collective-permute-done.3.refs_0_), channel_id=1, source_target_pairs={{0,12},{4,8},{8,4},{12,0},{1,13},{5,9},{9,5},{13,1},{2,14},{6,10},... | collective-permute-start | bytes 786440 | tf_op jit(solution)/shard_map/ppermute | solution.py:148
  47.4 22.8 %collective-permute-start.7 = (bf16[1024,640]{1,0:T(8,128)(2,1)S(1)}, bf16[1024,640]{1,0:T(8,128)(2,1)}, u32[]{:S(2)}, u32[]{:S(2)}) collective-permute-start(bf16[1024,640]{1,0:T(8,128)(2,1)S(1)} %constant_dynamic-update-slice_fusion.refs_4_), channel_id=1, source_target_pairs={{0,1},{1,0},{2,3},{3,2},{4,5},{5,4},{6,7},{7,6},{8,9},{9,8},{10,11... | collective-permute-start | bytes 3932168 | tf_op jit(solution)/shard_map/ppermute | solution.py:56
  49.6 16.5 %collective-permute-start.12 = (bf16[512,640]{1,0:T(8,128)(2,1)S(1)}, bf16[512,640]{1,0:T(8,128)(2,1)S(1)}, u32[]{:S(2)}, u32[]{:S(2)}) collective-permute-start(bf16[512,640]{1,0:T(8,128)(2,1)S(1)} %slice.187), channel_id=1, source_target_pairs={{0,2},{2,0},{1,3},{3,1},{4,6},{6,4},{5,7},{7,5},{8,10},{10,8},{9,1... | collective-permute-start | bytes 1966088 | tf_op jit(solution)/shard_map/ppermute | solution.py:56
  52.7 16.2 %collective-permute-start.14 = (bf16[512,640]{1,0:T(8,128)(2,1)S(1)}, bf16[512,640]{1,0:T(8,128)(2,1)}, u32[]{:S(2)}, u32[]{:S(2)}) collective-permute-start(bf16[512,640]{1,0:T(8,128)(2,1)S(1)} %slice.188), channel_id=1, source_target_pairs={{0,16},{16,0},{1,17},{17,1},{2,18},{18,2},{3,19},{19,3},{4,20},{20... | collective-permute-start | bytes 1966088 | tf_op jit(solution)/shard_map/ppermute | solution.py:56
  58.6 13.6 %collective-permute-start.11 = (bf16[1024,640]{1,0:T(8,128)(2,1)}, bf16[1024,640]{1,0:T(8,128)(2,1)}, u32[]{:S(2)}, u32[]{:S(2)}) collective-permute-start(bf16[1024,640]{1,0:T(8,128)(2,1)} %collective-permute-done.10.refs_8_), channel_id=1, source_target_pairs={{0,1},{1,0},{2,3},{3,2},{4,5},{5,4},{6,7},{7,6},{8,9},{9,8},{10,11... | collective-permute-start | bytes 3932168 | tf_op jit(solution)/shard_map/ppermute | solution.py:56
  61.7 10.5 %collective-permute-start.9 = (bf16[1024,640]{1,0:T(8,128)(2,1)S(1)}, bf16[1024,640]{1,0:T(8,128)(2,1)}, u32[]{:S(2)}, u32[]{:S(2)}) collective-permute-start(bf16[1024,640]{1,0:T(8,128)(2,1)S(1)} %collective-permute-done.8.refs_6_), channel_id=1, source_target_pairs={{0,1},{1,0},{2,3},{3,2},{4,5},{5,4},{6,7},{7,6},{8,9},{9,8},{10,11... | collective-permute-start | bytes 3932168 | tf_op jit(solution)/shard_map/ppermute | solution.py:56
  66.1 4.1 %collective-permute-start.13 = (bf16[512,640]{1,0:T(8,128)(2,1)S(1)}, bf16[512,640]{1,0:T(8,128)(2,1)}, u32[]{:S(2)}, u32[]{:S(2)}) collective-permute-start(bf16[512,640]{1,0:T(8,128)(2,1)S(1)} %collective-permute-done.12.refs_10_), channel_id=1, source_target_pairs={{0,1},{1,0},{2,3},{3,2},{4,5},{5,4},{6,7},{7,6},{8,9},{9,8},{10,11... | collective-permute-start | bytes 1966088 | tf_op jit(solution)/shard_map/ppermute | solution.py:56
  81.7 53.0 %all-to-all-start.1 = ((bf16[16,16,2560]{2,1,0:T(8,128)(2,1)}), bf16[16,16,2560]{2,1,0:T(8,128)(2,1)S(1)}, u32[]{:S(2)}, u32[]{:S(2)}) async-start(bf16[16,16,2560]{2,1,0:T(8,128)(2,1)} %bitcast.7), calls=%async_computation.1 | async-start | bytes 2621440 | tf_op jit(solution)/shard_map/all_to_all | solution.py:168
  93.0 37.9 %collective-permute-start.17 = (bf16[512,1024]{1,0:T(8,128)(2,1)}, bf16[512,1024]{1,0:T(8,128)(2,1)S(1)}, u32[]{:S(2)}, u32[]{:S(2)}) collective-permute-start(bf16[512,1024]{1,0:T(8,128)(2,1)} %refs_1_.1), channel_id=1, source_target_pairs={{0,16},{16,0},{1,17},{17,1},{2,18},{18,2},{3,19},{19,3},{4,20},{20... | collective-permute-start | bytes 3145736 | tf_op jit(solution)/shard_map/ppermute | solution.py:56
  93.9 37.8 %collective-permute-start.19 = (bf16[512,1024]{1,0:T(8,128)(2,1)}, bf16[512,1024]{1,0:T(8,128)(2,1)S(1)}, u32[]{:S(2)}, u32[]{:S(2)}) collective-permute-start(bf16[512,1024]{1,0:T(8,128)(2,1)} %refs_1_.1), channel_id=1, source_target_pairs={{0,2},{2,0},{1,3},{3,1},{4,6},{6,4},{5,7},{7,5},{8,10},{10,8},{9,1... | collective-permute-start | bytes 3145736 | tf_op jit(solution)/shard_map/ppermute | solution.py:56
  93.9 68.9 %collective-permute-start.16 = (bf16[512,1024]{1,0:T(8,128)(2,1)}, bf16[512,1024]{1,0:T(8,128)(2,1)}, u32[]{:S(2)}, u32[]{:S(2)}) collective-permute-start(bf16[512,1024]{1,0:T(8,128)(2,1)} %refs_1_.1), channel_id=1, source_target_pairs={{0,1},{1,0},{2,3},{3,2},{4,5},{5,4},{6,7},{7,6},{8,9},{9,8},{10,11... | collective-permute-start | bytes 3145736 | tf_op jit(solution)/shard_map/ppermute | solution.py:56
  131.7 30.0 %collective-permute-start.21 = (bf16[256,1024]{1,0:T(8,128)(2,1)}, bf16[256,1024]{1,0:T(8,128)(2,1)}, u32[]{:S(2)}, u32[]{:S(2)}) collective-permute-start(bf16[256,1024]{1,0:T(8,128)(2,1)} %slice.225), channel_id=1, source_target_pairs={{0,2},{2,0},{1,3},{3,1},{4,6},{6,4},{5,7},{7,5},{8,10},{10,8},{9,1... | collective-permute-start | bytes 1572872 | tf_op jit(solution)/shard_map/ppermute | solution.py:56
  132.6 30.1 %collective-permute-start.23 = (bf16[256,1024]{1,0:T(8,128)(2,1)}, bf16[256,1024]{1,0:T(8,128)(2,1)}, u32[]{:S(2)}, u32[]{:S(2)}) collective-permute-start(bf16[256,1024]{1,0:T(8,128)(2,1)} %slice.226), channel_id=1, source_target_pairs={{0,16},{16,0},{1,17},{17,1},{2,18},{18,2},{3,19},{19,3},{4,20},{20... | collective-permute-start | bytes 1572872 | tf_op jit(solution)/shard_map/ppermute | solution.py:56
  133.3 32.7 %collective-permute-start.18 = (bf16[512,1024]{1,0:T(8,128)(2,1)S(1)}, bf16[512,1024]{1,0:T(8,128)(2,1)}, u32[]{:S(2)}, u32[]{:S(2)}) collective-permute-start(bf16[512,1024]{1,0:T(8,128)(2,1)S(1)} %collective-permute-done.17.refs_3_), channel_id=1, source_target_pairs={{0,1},{1,0},{2,3},{3,2},{4,5},{5,4},{6,7},{7,6},{8,9},{9,8},{10,11... | collective-permute-start | bytes 3145736 | tf_op jit(solution)/shard_map/ppermute | solution.py:56
  134.7 31.3 %collective-permute-start.20 = (bf16[512,1024]{1,0:T(8,128)(2,1)S(1)}, bf16[512,1024]{1,0:T(8,128)(2,1)}, u32[]{:S(2)}, u32[]{:S(2)}) collective-permute-start(bf16[512,1024]{1,0:T(8,128)(2,1)S(1)} %collective-permute-done.19.refs_5_), channel_id=1, source_target_pairs={{0,1},{1,0},{2,3},{3,2},{4,5},{5,4},{6,7},{7,6},{8,9},{9,8},{10,11... | collective-permute-start | bytes 3145736 | tf_op jit(solution)/shard_map/ppermute | solution.py:56
  152.3 28.4 %all-to-all-start.2 = ((bf16[16,16,2048]{2,1,0:T(8,128)(2,1)}), bf16[16,16,2048]{2,1,0:T(8,128)(2,1)S(1)}, u32[]{:S(2)}, u32[]{:S(2)}) async-start(bf16[16,16,2048]{2,1,0:T(8,128)(2,1)} %bitcast.170), calls=%async_computation.2 | async-start | bytes 2097152 | tf_op jit(solution)/shard_map/all_to_all | solution.py:185
  203.9 5.8 %collective-permute-start.25 = (bf16[64,2048]{1,0:T(8,128)(2,1)S(1)}, bf16[64,2048]{1,0:T(8,128)(2,1)S(1)}, u32[]{:S(2)}, u32[]{:S(2)}) collective-permute-start(bf16[64,2048]{1,0:T(8,128)(2,1)S(1)} %reduce_sum.51), channel_id=1, source_target_pairs={{0,32},{4,0},{8,96},{12,64},{32,36},{36,4},{40,100},{44,68},{64,40... | collective-permute-start | bytes 786440 | tf_op jit(solution)/shard_map/ppermute | solution.py:208
  209.9 11.6 %collective-permute-start.26 = (f32[64]{0:T(128)S(1)}, f32[64]{0:T(128)S(1)}, u32[]{:S(2)}, u32[]{:S(2)}) collective-permute-start(f32[64]{0:T(128)S(1)} %multiply_reduce_fusion), channel_id=1, source_target_pairs={{0,4},{4,0},{8,12},{12,8},{1,5},{5,1},{9,13},{13,9},{2,6},{6,2},{1... | collective-permute-start | bytes 776 | tf_op jit(solution)/shard_map/ppermute | solution.py:121
  211.2 10.3 %collective-permute-start.27 = (f32[64]{0:T(128)S(1)}, f32[64]{0:T(128)S(1)}, u32[]{:S(2)}, u32[]{:S(2)}) collective-permute-start(f32[64]{0:T(128)S(1)} %multiply_reduce_fusion), channel_id=1, source_target_pairs={{0,8},{4,12},{8,0},{12,4},{1,9},{5,13},{9,1},{13,5},{2,10},{6,14},... | collective-permute-start | bytes 776 | tf_op jit(solution)/shard_map/ppermute | solution.py:121
  (26 other events, 126.3 us)
where the time goes:
time: 241 us; the launch traced here: 239 us
  starting transfers between devices  89 us (37%)
  waiting for transfers between devices  73 us (30%)
  blocking collectives  28.9 us (12%)
  local copies, waits for them, and re-layouts  18.2 us (8%)
  Pallas kernels  11.7 us (5%)
  matrix products  8.75 us (4%)
  other arithmetic  8.43 us (3%)
    ppermute x18, waiting for transfers between devices, swap(): return lax.ppermute(v, axis, FLIP)  43.9 us
    ppermute x3, starting transfers between devices, local(): lax.ppermute(normed, 'x', xor_pairs(k))  26.5 us
    ppermute x18, starting transfers between devices, swap(): return lax.ppermute(v, axis, FLIP)  19.5 us
    all_to_all x1, blocking collectives, local(): out = lax.all_to_all(out, 'x', 0, 0, tiled=True)  15.8 us
    all_to_all x1, waiting for transfers between devices, local(): lax.all_to_all(context, WIDE, 0, 0, tiled=True).reshape(tokens, wide)  14.7 us
    ppermute x6, starting transfers between devices, sum_over_x(): return sum((lax.ppermute(v, 'x', xor_pairs(k)) for k in (1, 2, 3)), v)  14.6 us
    all_to_all x1, blocking collectives, local(): both = lax.all_to_all(both, PAIR, 0, 0, tiled=True)  13.1 us
    pallas_call x2, Pallas kernels, matmul_kernel(): pl.pallas_call(body, out_shape=jax.ShapeDtypeStruct(out_shape, BF16), in_...  11.7 us
  transfers between devices with their start and end apart: 32, of which 12 were waited for; matrix products, arithmetic and copies ran while one was open for 9% of the time, Pallas kernels for 0%

commit v1 on v0

--- a/solution.py
+++ b/solution.py
@@ -48,8 +48,10 @@
 
 
 SPREAD = [(g * 4 + x, x * 4 + (g ^ x)) for g in range(4) for x in range(4)]
-COLLECT = [(g * 4 + x, (x ^ 1) * 4 + g) for g in range(4) for x in range(4)]
 FLIP = [(0, 1), (1, 0)]
+CHIP = ("x", "yl")
+BLOCK = ("yh", "zh", "zl")
+ACROSS = ("yh", "zh", "zl", "yl")
 
 
 def swap(v, axis):
@@ -66,6 +68,16 @@
     return pieces
 
 
+def row_of(w):
+    near = {k: lax.ppermute(w, "x", xor_pairs(k)) for k in (1, 3)}
+    near[2] = lax.ppermute(w, "x", xor_pairs(2))
+    near[0] = w
+    pieces = []
+    for k in (0, 1, 3, 2):
+        pieces += [(k, 0, near[k]), (k, 1, swap(near[k], "c"))]
+    return pieces
+
+
 def matmul_kernel(lhs_pieces, weights, out_shape, place, finish, scalars):
     n = len(weights)
 
@@ -76,15 +88,22 @@
         copies = [pltpu.make_async_copy(w_refs[i], bufs[i], sem.at[i]) for i in range(n)]
         for copy in copies:
             copy.start()
-        place(scalar_ref, lhs_refs, lhs_scr)
+        if place is None:
+            lhs_scr = lhs_refs[0]
+        else:
+            place(scalar_ref, lhs_refs, lhs_scr)
         slots = sorted({slot for _, slot, _ in weights})
         for slot in slots:
             acc = None
-            for i, (col, at, w) in enumerate(weights):
-                if at != slot:
+            for i, (col, home, w) in enumerate(weights):
+                if home != slot:
                     continue
                 copies[i].wait()
-                term = jnp.dot(lhs_scr[:, col : col + w.shape[0]], bufs[i][...], preferred_element_type=F32)
+                if callable(col):
+                    at = pl.ds(pl.multiple_of(col(scalar_ref), 128), w.shape[0])
+                else:
+                    at = slice(col, col + w.shape[0])
+                term = jnp.dot(lhs_scr[:, at], bufs[i][...], preferred_element_type=F32)
                 acc = term if acc is None else acc + term
             finish(scalar_ref, out_ref, slot, acc.astype(BF16))
 
@@ -98,7 +117,7 @@
         + [pl.BlockSpec(memory_space=pltpu.VMEM)] * len(lhs_pieces)
         + [pl.BlockSpec(memory_space=pltpu.HBM)] * n,
         out_specs=pl.BlockSpec(memory_space=pltpu.VMEM),
-        scratch_shapes=[pltpu.VMEM((rows, depth), BF16)]
+        scratch_shapes=[pltpu.VMEM((rows, depth) if place else (8, 128), BF16)]
         + [pltpu.VMEM(w.shape, BF16) for _, _, w in weights]
         + [pltpu.SemaphoreType.DMA((n,))],
         compiler_params=pltpu.CompilerParams(vmem_limit_bytes=30 << 20),
@@ -133,10 +152,15 @@
     q_cols = w_query.shape[1]
     rows, cols = w_query.shape[0], q_cols + w_keyval.shape[1]
     w_qkv = cube_of(jnp.concatenate([w_query, w_keyval], axis=1))
-    w_out = cube_of(w_output)
+    w_out = row_of(w_output)
 
     sent = h.reshape(4, 4, seq_dev, width).transpose(1, 0, 2, 3).reshape(4, quarter, width)
     got = lax.all_to_all(sent, PAIR, 0, 0, tiled=True)
+    core = lax.axis_index("c")
+    by_core = h.reshape(8, 2, seq_dev, width)
+    mine = lax.dynamic_index_in_dim(by_core, core, 1, keepdims=False).reshape(-1, width)
+    other = swap(lax.dynamic_index_in_dim(by_core, 1 - core, 1, keepdims=False), "c").reshape(-1, width)
+    home_rows = jnp.concatenate(unrelated([mine, other], core), axis=1)
     resident = got.transpose(1, 0, 2).reshape(quarter, wide).astype(F32)
     squares = sum_over_x(jnp.sum(resident * resident, axis=1))
     inverse = lax.rsqrt(squares / model + EPS)[:, None]
@@ -180,40 +204,42 @@
     grouped = roped_q.reshape(seq_dev, kv_heads, per_kv, head_dim)
     context = attend(grouped, new_keys, new_values, cache_keys, cache_values, own_len)
 
-    context = context.reshape(seq_dev, 4, wide).transpose(1, 0, 2)
-    context = jnp.broadcast_to(context[None], (4, 4, seq_dev, wide)).reshape(16, seq_dev, wide)
-    context = lax.all_to_all(context, WIDE, 0, 0, tiled=True).reshape(tokens, wide)
-
-    def place_heads(scalar_ref, lhs_refs, lhs_scr):
-        for p in range(4):
-            at = pl.multiple_of((scalar_ref[0] ^ p) * width, width)
-            lhs_scr[:, p * width : (p + 1) * width] = lhs_refs[0][:, pl.ds(at, width)]
+    context = context.reshape(seq_dev, 4, 2, 2 * width).transpose(2, 0, 1, 3).reshape(1, 2, seq_dev, 2 * wide)
+    context = jnp.broadcast_to(context, (8, 2, seq_dev, 2 * wide)).reshape(16, seq_dev, 2 * wide)
+    context = lax.all_to_all(context, ACROSS, 0, 0, tiled=True).reshape(tokens, 2 * wide)
+    out_cols = w_output.shape[1]
+    chip = lax.axis_index(CHIP)
+    part = 2 * seq_dev
+
+    def column_of(dx, dc):
+        return lambda scalar_ref: ((scalar_ref[0] ^ dx) * 2 + (scalar_ref[1] ^ dc)) * width
 
     def put_blocks(scalar_ref, out_ref, slot, value):
-        n = value.shape[1]
-        at = pl.multiple_of((scalar_ref[1] ^ slot) * n, n)
-        for j in range(4):
-            out_ref[j ^ 1, :, pl.ds(at, n)] = value[j * quarter : (j + 1) * quarter]
+        for g in range(8):
+            out_ref[g] = value[g * part : (g + 1) * part]
 
     out = matmul_kernel(
         [context],
-        [((dy * 2 + dc) * width + row, dz, v) for dz, dy, dc, row, v in w_out],
-        (4, quarter, wide),
-        place_heads,
+        [(column_of(dx, dc), 0, v) for dx, dc, v in w_out],
+        (8, part, out_cols),
+        None,
         put_blocks,
-        [pair_pos, z_pos],
+        [x_pos, core],
     )
-    out = lax.all_to_all(out, "x", 0, 0, tiled=True)
-    out = jnp.sum(out.astype(F32), axis=0).astype(BF16)
-    branch = lax.ppermute(out, WIDE, COLLECT)
-    stream = resident + branch.astype(F32)
-    squares_two = sum_over_x(jnp.sum(stream * stream, axis=1))
-    inverse_two = lax.rsqrt(squares_two / model + EPS)[:, None]
-    gain_two = lax.dynamic_slice_in_dim(ffn_gain, x_pos * wide, wide).astype(F32)
+    out = lax.all_to_all(out, BLOCK, 0, 0, tiled=True)
+    out = lax.all_to_all(out, CHIP, 0, 0, tiled=True)
+    summed = jnp.sum(out.reshape(4, 2, part, out_cols).astype(F32), axis=1).reshape(tokens // 2, out_cols)
+    stream = home_rows.astype(F32) + summed
+    squares_two = jnp.sum(stream * stream, axis=1)
+    squares_two = lax.all_to_all(jnp.broadcast_to(squares_two[None], (8, tokens // 2)), CHIP, 0, 0, tiled=True)
+    inverse_two = lax.rsqrt(jnp.sum(squares_two, axis=0) / model + EPS)[:, None]
+    gain_two = lax.dynamic_slice_in_dim(ffn_gain, chip * out_cols, out_cols).astype(F32)
     ffn_input = (stream * inverse_two * gain_two).astype(BF16)
-    both = jnp.stack([branch, ffn_input]).reshape(2, quarter, 4, width).transpose(2, 0, 1, 3)
-    both = lax.all_to_all(both, PAIR, 0, 0, tiled=True)
-    both = both.reshape(4, 2, 4, seq_dev, width).transpose(1, 2, 0, 3, 4).reshape(2, tokens, width)
+    both = jnp.stack([summed.astype(BF16), ffn_input]).reshape(2, tokens // 2, 2, width)
+    keep = lax.dynamic_index_in_dim(both, core, 2, keepdims=False)
+    came = swap(lax.dynamic_index_in_dim(both, 1 - core, 2, keepdims=False), "c")
+    both = unrelated([v.reshape(2, 8, seq_dev, width) for v in (keep, came)], core)
+    both = jnp.stack(both, axis=2).reshape(2, tokens, width)
     return both[0], both[1]
 
 

time: 241 us -> 219 us (0.909)
  blocking collectives: 28.9 us -> 0 us
  starting transfers between devices: 89 us -> 95.9 us
  local copies, waits for them, and re-layouts: 18.2 us -> 22.8 us
    ppermute x18 -> x15, waiting for transfers between devices: 43.9 us -> 7.87 us  [swap(): return lax.ppermute(v, axis, FLIP)]
    all_to_all x2 -> x0, blocking collectives: 28.9 us -> none  [the longest x1 15.8 us: local(): out = lax.all_to_all(out, 'x', 0, 0, tiled=True)]
    all_to_all x1, waiting for transfers between devices: 0.01 us -> 18.4 us  [local(): arrived = lax.all_to_all(partial, WIDE, 0, 0, tiled=True)]
    ppermute x1 -> x3, waiting for transfers between devices: 3.74 us -> 20.6 us  [the longest x1 20.6 us: row_of(): near[2] = lax.ppermute(w, 'x', xor_pairs(2))]
    ppermute x6 -> x3, starting transfers between devices: 14.6 us -> 3.93 us  [sum_over_x(): return sum((lax.ppermute(v, 'x', xor_pairs(k)) for k in (1, 2, 3)), v)]
    all_to_all x1 -> x4, starting transfers between devices: 9.44 us -> 17.8 us  [the longest x1 6.58 us: local(): out = lax.all_to_all(out, BLOCK, 0, 0, tiled=True)]
    ppermute x18 -> x15, starting transfers between devices: 19.5 us -> 26.8 us  [swap(): return lax.ppermute(v, axis, FLIP)]
    unnamed x37 -> x45, local copies, waits for them, and re-layouts: 9.49 us -> 14 us
  transfers between devices with their start and end apart: 32 -> 31, of which waited for: 12 -> 14; matrix products, arithmetic and copies ran while one was open for 9% -> 8% of each run, Pallas kernels for 0% -> 0%
where the time goes in v1:
time: 219 us; the launch traced here: 218 us
  starting transfers between devices  95.9 us (44%)
  waiting for transfers between devices  71.4 us (33%)
  local copies, waits for them, and re-layouts  22.8 us (10%)
  Pallas kernels  11.4 us (5%)
  matrix products  8.75 us (4%)
  other arithmetic  6.09 us (3%)
    ppermute x15, starting transfers between devices, swap(): return lax.ppermute(v, axis, FLIP)  26.8 us
    ppermute x3, starting transfers between devices, local(): lax.ppermute(normed, 'x', xor_pairs(k))  26.5 us
    ppermute x1, waiting for transfers between devices, row_of(): near[2] = lax.ppermute(w, 'x', xor_pairs(2))  20.6 us
    all_to_all x1, waiting for transfers between devices, local(): arrived = lax.all_to_all(partial, WIDE, 0, 0, tiled=True)  18.4 us
    unnamed x45, local copies, waits for them, and re-layouts  14 us
    all_to_all x1, starting transfers between devices, local(): arrived = lax.all_to_all(partial, WIDE, 0, 0, tiled=True)  11.5 us
    pallas_call x2, Pallas kernels, matmul_kernel(): pl.pallas_call(body, out_shape=jax.ShapeDtypeStruct(out_shape, BF16), in_...  11.4 us
    all_to_all x1, waiting for transfers between devices, local(): out = lax.all_to_all(out, BLOCK, 0, 0, tiled=True)  9.21 us
  transfers between devices with their start and end apart: 31, of which 14 were waited for; matrix products, arithmetic and copies ran while one was open for 8% of the time, Pallas kernels for 0%

profile of v1, /device:TPU:1, one launch (start us, length us, event | category | flops | bytes accessed | tf_op | source)
XLA Modules:
  0.0 217.6 jit_solution(16820938792631246171)
XLA Ops:
  2.4 4.9 %all-to-all-start = ((bf16[4,64,512]{2,1,0:T(8,128)(2,1)}), bf16[4,64,512]{2,1,0:T(8,128)(2,1)S(1)}, u32[]{:S(2)}, u32[]{:S(2)}) async-start(bf16[4,64,512]{2,1,0:T(8,128)(2,1)} %bitcast.5), calls=%async_computation | async-start | bytes 524288 | tf_op jit(solution)/shard_map/all_to_all | solution.py:158
  13.9 2.5 %collective-permute-start.1 = (f32[64]{0:T(128)S(1)}, f32[64]{0:T(128)S(1)}, u32[]{:S(2)}, u32[]{:S(2)}) collective-permute-start(f32[64]{0:T(128)S(1)} %fusion.3), channel_id=1, source_target_pairs={{0,8},{4,12},{8,0},{12,4},{1,9},{5,13},{9,1},{13,5},{2,10},{6,14},... | collective-permute-start | bytes 776 | tf_op jit(solution)/shard_map/ppermute | solution.py:140
  17.8 2.2 collective-permute-done.2
  20.8 23.3 %collective-permute-start.4 = (bf16[64,2048]{1,0:T(8,128)(2,1)S(1)}, bf16[64,2048]{1,0:T(8,128)(2,1)S(1)}, u32[]{:S(2)}, u32[]{:S(2)}) collective-permute-start(bf16[64,2048]{1,0:T(8,128)(2,1)S(1)} %collective-permute-done.3.refs_0_), channel_id=1, source_target_pairs={{0,4},{4,0},{8,12},{12,8},{1,5},{5,1},{9,13},{13,9},{2,6},{6,2},{1... | collective-permute-start | bytes 786440 | tf_op jit(solution)/shard_map/ppermute | solution.py:172
  44.2 3.2 %collective-permute-start.5 = (bf16[64,2048]{1,0:T(8,128)(2,1)S(1)}, bf16[64,2048]{1,0:T(8,128)(2,1)S(1)}, u32[]{:S(2)}, u32[]{:S(2)}) collective-permute-start(bf16[64,2048]{1,0:T(8,128)(2,1)S(1)} %collective-permute-done.3.refs_0_), channel_id=1, source_target_pairs={{0,8},{4,12},{8,0},{12,4},{1,9},{5,13},{9,1},{13,5},{2,10},{6,14},... | collective-permute-start | bytes 786440 | tf_op jit(solution)/shard_map/ppermute | solution.py:172
  54.3 3.6 %collective-permute-done.5.refs_2_ = bf16[64,2048]{1,0:T(8,128)(2,1)S(1)} collective-permute-done((bf16[64,2048]{1,0:T(8,128)(2,1)S(1)}, bf16[64,2048]{1,0:T(8,128)(2,1)S(1)}, u32[]{:S(2)}, u32[]{:S(2)}) %collective-permute-start.5) | collective-permute-done | bytes 262176 | tf_op jit(solution)/shard_map/ppermute | solution.py:172
  58.6 2.4 %collective-permute-start.11 = (bf16[1024,640]{1,0:T(8,128)(2,1)}, bf16[1024,640]{1,0:T(8,128)(2,1)}, u32[]{:S(2)}, u32[]{:S(2)}) collective-permute-start(bf16[1024,640]{1,0:T(8,128)(2,1)} %collective-permute-done.10.refs_8_), channel_id=1, source_target_pairs={{0,1},{1,0},{2,3},{3,2},{4,5},{5,4},{6,7},{7,6},{8,9},{9,8},{10,11... | collective-permute-start | bytes 3932168 | tf_op jit(solution)/shard_map/ppermute | solution.py:58
  63.6 2.4 %collective-permute-done.12.refs_10_ = bf16[512,640]{1,0:T(8,128)(2,1)S(1)} collective-permute-done((bf16[512,640]{1,0:T(8,128)(2,1)S(1)}, bf16[512,640]{1,0:T(8,128)(2,1)S(1)}, u32[]{:S(2)}, u32[]{:S(2)}) %collective-permute-start.12) | collective-permute-done | bytes 655392 | tf_op jit(solution)/shard_map/ppermute | solution.py:58
  75.0 6.5 %shard_map.104 = bf16[256,2560]{1,0:T(8,128)(2,1)} custom-call(s32[1]{0:T(128)} %bitcast.2.scalar_ref, bf16[64,2048]{1,0:T(8,128)(2,1)S(1)} %collective-permute-done.3.refs_0_, bf16[64,2048]{1,0:T(8,128)(2,1)S(1)} %copy-done.10, bf16[64,2048]{1,0:T(8,128)(2,1)S(1)} %copy-done.12, bf16[64,2048]{1,0:T(8,128)(2,1)S(1)} %copy-done.14, ...), custom_call_target="tpu_custom_call" | custom-call | flops 2684354560 | bytes 10485760 | tf_op jit(solution)/shard_map/pallas_call | solution.py:113
  81.6 11.5 %all-to-all-start.1 = ((bf16[16,16,2560]{2,1,0:T(8,128)(2,1)}), bf16[16,16,2560]{2,1,0:T(8,128)(2,1)S(1)}, u32[]{:S(2)}, u32[]{:S(2)}) async-start(bf16[16,16,2560]{2,1,0:T(8,128)(2,1)} %bitcast.7), calls=%async_computation.1 | async-start | bytes 2621440 | tf_op jit(solution)/shard_map/all_to_all | solution.py:192
  97.2 18.4 %all-to-all-done.1 = bf16[16,16,2560]{2,1,0:T(8,128)(2,1)S(1)} async-done(((bf16[16,16,2560]{2,1,0:T(8,128)(2,1)}), bf16[16,16,2560]{2,1,0:T(8,128)(2,1)S(1)}, u32[]{:S(2)}, u32[]{:S(2)}) %all-to-all-start.1) | async-done | bytes 1310752 | tf_op jit(solution)/shard_map/all_to_all | solution.py:192
  117.8 6.6 %fusion.27 = (f32[16,8,8]{2,1,0:T(8,128)S(1)}, f32[16,8,8,192]{3,2,1,0:T(8,128)S(1)}) fusion(bf16[16,8,192,128]{3,2,1,0:T(8,128)(2,1)} %param.15, bf16[16,8,8,64]{3,2,1,0:T(8,128)(2,1)S(1)} %get-tuple-element.31, bf16[16,8,8,64]{3,2,1,0:T(8,128)(2,1)S(1)} %get-tuple-element.30, pred[16,192]{1,0:T(8,128)(4,1)S(1)} %iota_compare_fusion), kind=kOutput, calls=%fused_computation.132 | convolution fusion | flops 51444736 | bytes 7347200 | tf_op jit(solution)/shard_map/nkgd,nkld->nkgl/dot_general | solution.py:31
  128.7 3.7 %all-to-all-start.2 = ((bf16[16,16,4096]{2,1,0:T(8,128)(2,1)}), bf16[16,16,4096]{2,1,0:T(8,128)(2,1)S(1)}, u32[]{:S(2)}, u32[]{:S(2)}) async-start(bf16[16,16,4096]{2,1,0:T(8,128)(2,1)} %bitcast.189), calls=%async_computation.2 | async-start | bytes 4194304 | tf_op jit(solution)/shard_map/all_to_all | solution.py:209
  132.4 2.9 %collective-permute-start.16 = (bf16[512,1024]{1,0:T(8,128)(2,1)S(1)}, bf16[512,1024]{1,0:T(8,128)(2,1)S(1)}, u32[]{:S(2)}, u32[]{:S(2)}) collective-permute-start(bf16[512,1024]{1,0:T(8,128)(2,1)S(1)} %copy-done), channel_id=1, source_target_pairs={{0,1},{1,0},{2,3},{3,2},{4,5},{5,4},{6,7},{7,6},{8,9},{9,8},{10,11... | collective-permute-start | bytes 3145736 | tf_op jit(solution)/shard_map/ppermute | solution.py:58
  135.8 20.6 %collective-permute-done.21.refs_7_ = bf16[512,1024]{1,0:T(8,128)(2,1)} collective-permute-done((bf16[512,1024]{1,0:T(8,128)(2,1)S(1)}, bf16[512,1024]{1,0:T(8,128)(2,1)}, u32[]{:S(2)}, u32[]{:S(2)}) %collective-permute-start.21) | collective-permute-done | bytes 1048608 | tf_op jit(solution)/shard_map/ppermute | solution.py:73
  166.9 4.8 %shard_map.105 = bf16[8,32,1024]{2,1,0:T(8,128)(2,1)} custom-call(s32[2]{0:T(128)S(1)} %pad_add_fusion.scalar_ref, bf16[256,4096]{1,0:T(8,128)(2,1)S(1)} %bitcast.188, bf16[512,1024]{1,0:T(8,128)(2,1)S(1)} %copy-done, bf16[512,1024]{1,0:T(8,128)(2,1)S(1)} %copy-done.2, bf16[512,1024]{1,0:T(8,128)(2,1)} %collective-permute-done.17.refs_3_, ...), custom_call_target="tpu_custom_call" | custom-call | flops 2147483648 | bytes 8388608 | tf_op jit(solution)/shard_map/pallas_call | solution.py:113
  171.7 6.6 %all-to-all-start.3 = ((bf16[8,32,1024]{2,1,0:T(8,128)(2,1)}), bf16[8,32,1024]{2,1,0:T(8,128)(2,1)}, u32[]{:S(2)}, u32[]{:S(2)}) async-start(bf16[8,32,1024]{2,1,0:T(8,128)(2,1)} %shard_map.105), calls=%async_computation.3 | async-start | bytes 1048576 | tf_op jit(solution)/shard_map/all_to_all | solution.py:229
  178.3 9.2 %all-to-all-done.3 = bf16[8,32,1024]{2,1,0:T(8,128)(2,1)} async-done(((bf16[8,32,1024]{2,1,0:T(8,128)(2,1)}), bf16[8,32,1024]{2,1,0:T(8,128)(2,1)}, u32[]{:S(2)}, u32[]{:S(2)}) %all-to-all-start.3) | async-done | bytes 524320 | tf_op jit(solution)/shard_map/all_to_all | solution.py:229
  187.5 4.0 %all-to-all-start.4 = ((bf16[8,32,1024]{2,1,0:T(8,128)(2,1)}), bf16[8,32,1024]{2,1,0:T(8,128)(2,1)S(1)}, u32[]{:S(2)}, u32[]{:S(2)}) async-start(bf16[8,32,1024]{2,1,0:T(8,128)(2,1)} %all-to-all-done.3), calls=%async_computation.4 | async-start | bytes 1048576 | tf_op jit(solution)/shard_map/all_to_all | solution.py:230
  191.5 2.6 %collective-permute-start.23 = (bf16[8,16,512]{2,1,0:T(8,128)(2,1)S(1)}, bf16[8,16,512]{2,1,0:T(8,128)(2,1)S(1)}, u32[]{:S(2)}, u32[]{:S(2)}) collective-permute-start(bf16[8,16,512]{2,1,0:T(8,128)(2,1)S(1)} %get-tuple-element.44), channel_id=1, source_target_pairs={{0,1},{1,0},{2,3},{3,2},{4,5},{5,4},{6,7},{7,6},{8,9},{9,8},{10,11... | collective-permute-start | bytes 393224 | tf_op jit(solution)/shard_map/ppermute | solution.py:58
  195.1 3.5 %all-to-all-done.4 = bf16[8,32,1024]{2,1,0:T(8,128)(2,1)S(1)} async-done(((bf16[8,32,1024]{2,1,0:T(8,128)(2,1)}), bf16[8,32,1024]{2,1,0:T(8,128)(2,1)S(1)}, u32[]{:S(2)}, u32[]{:S(2)}) %all-to-all-start.4) | async-done | bytes 524320 | tf_op jit(solution)/shard_map/all_to_all | solution.py:230
  199.6 3.5 %all-to-all-start.5 = ((f32[8,1,128]{2,1,0:T(1,128)}), f32[8,1,128]{2,1,0:T(1,128)S(1)}, u32[]{:S(2)}, u32[]{:S(2)}) async-start(f32[8,1,128]{2,1,0:T(1,128)} %broadcast_in_dim.25), calls=%async_computation.5 | async-start | bytes 8192 | tf_op jit(solution)/shard_map/all_to_all | solution.py:234
  204.0 3.7 %all-to-all-done.5 = f32[8,1,128]{2,1,0:T(1,128)S(1)} async-done(((f32[8,1,128]{2,1,0:T(1,128)}), f32[8,1,128]{2,1,0:T(1,128)S(1)}, u32[]{:S(2)}, u32[]{:S(2)}) %all-to-all-start.5) | async-done | bytes 4128 | tf_op jit(solution)/shard_map/all_to_all | solution.py:234
  210.1 4.8 %collective-permute-start.24 = (bf16[2,128,512]{2,1,0:T(8,128)(2,1)S(1)}, bf16[2,128,512]{2,1,0:T(8,128)(2,1)S(1)}, u32[]{:S(2)}, u32[]{:S(2)}) collective-permute-start(bf16[2,128,512]{2,1,0:T(8,128)(2,1)S(1)} %bitcast.201), channel_id=1, source_target_pairs={{0,1},{1,0},{2,3},{3,2},{4,5},{5,4},{6,7},{7,6},{8,9},{9,8},{10,11... | collective-permute-start | bytes 786440 | tf_op jit(solution)/shard_map/ppermute | solution.py:58
  (169 shorter events, 58.9 us)
Async XLA Ops:
  2.4 9.9 %all-to-all-start = ((bf16[4,64,512]{2,1,0:T(8,128)(2,1)}), bf16[4,64,512]{2,1,0:T(8,128)(2,1)S(1)}, u32[]{:S(2)}, u32[]{:S(2)}) async-start(bf16[4,64,512]{2,1,0:T(8,128)(2,1)} %bitcast.5), calls=%async_computation | async-start | bytes 524288 | tf_op jit(solution)/shard_map/all_to_all | solution.py:158
  7.4 39.9 %collective-permute-start.8 = (bf16[1024,640]{1,0:T(8,128)(2,1)S(1)}, bf16[1024,640]{1,0:T(8,128)(2,1)S(1)}, u32[]{:S(2)}, u32[]{:S(2)}) collective-permute-start(bf16[1024,640]{1,0:T(8,128)(2,1)S(1)} %constant_dynamic-update-slice_fusion.refs_4_), channel_id=1, source_target_pairs={{0,16},{16,0},{1,17},{17,1},{2,18},{18,2},{3,19},{19,3},{4,20},{20... | collective-permute-start | bytes 3932168 | tf_op jit(solution)/shard_map/ppermute | solution.py:58
  9.3 40.3 %collective-permute-start.10 = (bf16[1024,640]{1,0:T(8,128)(2,1)S(1)}, bf16[1024,640]{1,0:T(8,128)(2,1)}, u32[]{:S(2)}, u32[]{:S(2)}) collective-permute-start(bf16[1024,640]{1,0:T(8,128)(2,1)S(1)} %constant_dynamic-update-slice_fusion.refs_4_), channel_id=1, source_target_pairs={{0,2},{2,0},{1,3},{3,1},{4,6},{6,4},{5,7},{7,5},{8,10},{10,8},{9,1... | collective-permute-start | bytes 3932168 | tf_op jit(solution)/shard_map/ppermute | solution.py:58
  20.8 31.1 %collective-permute-start.4 = (bf16[64,2048]{1,0:T(8,128)(2,1)S(1)}, bf16[64,2048]{1,0:T(8,128)(2,1)S(1)}, u32[]{:S(2)}, u32[]{:S(2)}) collective-permute-start(bf16[64,2048]{1,0:T(8,128)(2,1)S(1)} %collective-permute-done.3.refs_0_), channel_id=1, source_target_pairs={{0,4},{4,0},{8,12},{12,8},{1,5},{5,1},{9,13},{13,9},{2,6},{6,2},{1... | collective-permute-start | bytes 786440 | tf_op jit(solution)/shard_map/ppermute | solution.py:172
  44.2 13.7 %collective-permute-start.5 = (bf16[64,2048]{1,0:T(8,128)(2,1)S(1)}, bf16[64,2048]{1,0:T(8,128)(2,1)S(1)}, u32[]{:S(2)}, u32[]{:S(2)}) collective-permute-start(bf16[64,2048]{1,0:T(8,128)(2,1)S(1)} %collective-permute-done.3.refs_0_), channel_id=1, source_target_pairs={{0,8},{4,12},{8,0},{12,4},{1,9},{5,13},{9,1},{13,5},{2,10},{6,14},... | collective-permute-start | bytes 786440 | tf_op jit(solution)/shard_map/ppermute | solution.py:172
  47.4 13.7 %collective-permute-start.6 = (bf16[64,2048]{1,0:T(8,128)(2,1)S(1)}, bf16[64,2048]{1,0:T(8,128)(2,1)S(1)}, u32[]{:S(2)}, u32[]{:S(2)}) collective-permute-start(bf16[64,2048]{1,0:T(8,128)(2,1)S(1)} %collective-permute-done.3.refs_0_), channel_id=1, source_target_pairs={{0,12},{4,8},{8,4},{12,0},{1,13},{5,9},{9,5},{13,1},{2,14},{6,10},... | collective-permute-start | bytes 786440 | tf_op jit(solution)/shard_map/ppermute | solution.py:172
  47.4 22.7 %collective-permute-start.7 = (bf16[1024,640]{1,0:T(8,128)(2,1)S(1)}, bf16[1024,640]{1,0:T(8,128)(2,1)}, u32[]{:S(2)}, u32[]{:S(2)}) collective-permute-start(bf16[1024,640]{1,0:T(8,128)(2,1)S(1)} %constant_dynamic-update-slice_fusion.refs_4_), channel_id=1, source_target_pairs={{0,1},{1,0},{2,3},{3,2},{4,5},{5,4},{6,7},{7,6},{8,9},{9,8},{10,11... | collective-permute-start | bytes 3932168 | tf_op jit(solution)/shard_map/ppermute | solution.py:58
  49.5 16.5 %collective-permute-start.12 = (bf16[512,640]{1,0:T(8,128)(2,1)S(1)}, bf16[512,640]{1,0:T(8,128)(2,1)S(1)}, u32[]{:S(2)}, u32[]{:S(2)}) collective-permute-start(bf16[512,640]{1,0:T(8,128)(2,1)S(1)} %slice.179), channel_id=1, source_target_pairs={{0,2},{2,0},{1,3},{3,1},{4,6},{6,4},{5,7},{7,5},{8,10},{10,8},{9,1... | collective-permute-start | bytes 1966088 | tf_op jit(solution)/shard_map/ppermute | solution.py:58
  52.6 16.1 %collective-permute-start.14 = (bf16[512,640]{1,0:T(8,128)(2,1)S(1)}, bf16[512,640]{1,0:T(8,128)(2,1)}, u32[]{:S(2)}, u32[]{:S(2)}) collective-permute-start(bf16[512,640]{1,0:T(8,128)(2,1)S(1)} %slice.180), channel_id=1, source_target_pairs={{0,16},{16,0},{1,17},{17,1},{2,18},{18,2},{3,19},{19,3},{4,20},{20... | collective-permute-start | bytes 1966088 | tf_op jit(solution)/shard_map/ppermute | solution.py:58
  58.6 13.5 %collective-permute-start.11 = (bf16[1024,640]{1,0:T(8,128)(2,1)}, bf16[1024,640]{1,0:T(8,128)(2,1)}, u32[]{:S(2)}, u32[]{:S(2)}) collective-permute-start(bf16[1024,640]{1,0:T(8,128)(2,1)} %collective-permute-done.10.refs_8_), channel_id=1, source_target_pairs={{0,1},{1,0},{2,3},{3,2},{4,5},{5,4},{6,7},{7,6},{8,9},{9,8},{10,11... | collective-permute-start | bytes 3932168 | tf_op jit(solution)/shard_map/ppermute | solution.py:58
  61.8 10.4 %collective-permute-start.9 = (bf16[1024,640]{1,0:T(8,128)(2,1)S(1)}, bf16[1024,640]{1,0:T(8,128)(2,1)}, u32[]{:S(2)}, u32[]{:S(2)}) collective-permute-start(bf16[1024,640]{1,0:T(8,128)(2,1)S(1)} %collective-permute-done.8.refs_6_), channel_id=1, source_target_pairs={{0,1},{1,0},{2,3},{3,2},{4,5},{5,4},{6,7},{7,6},{8,9},{9,8},{10,11... | collective-permute-start | bytes 3932168 | tf_op jit(solution)/shard_map/ppermute | solution.py:58
  81.6 34.1 %all-to-all-start.1 = ((bf16[16,16,2560]{2,1,0:T(8,128)(2,1)}), bf16[16,16,2560]{2,1,0:T(8,128)(2,1)S(1)}, u32[]{:S(2)}, u32[]{:S(2)}) async-start(bf16[16,16,2560]{2,1,0:T(8,128)(2,1)} %bitcast.7), calls=%async_computation.1 | async-start | bytes 2621440 | tf_op jit(solution)/shard_map/all_to_all | solution.py:192
  93.1 42.2 %collective-permute-start.17 = (bf16[512,1024]{1,0:T(8,128)(2,1)S(1)}, bf16[512,1024]{1,0:T(8,128)(2,1)}, u32[]{:S(2)}, u32[]{:S(2)}) collective-permute-start(bf16[512,1024]{1,0:T(8,128)(2,1)S(1)} %copy-done), channel_id=1, source_target_pairs={{0,4},{4,0},{8,12},{12,8},{1,5},{5,1},{9,13},{13,9},{2,6},{6,2},{1... | collective-permute-start | bytes 3145736 | tf_op jit(solution)/shard_map/ppermute | solution.py:72
  94.5 40.9 %collective-permute-start.19 = (bf16[512,1024]{1,0:T(8,128)(2,1)S(1)}, bf16[512,1024]{1,0:T(8,128)(2,1)}, u32[]{:S(2)}, u32[]{:S(2)}) collective-permute-start(bf16[512,1024]{1,0:T(8,128)(2,1)S(1)} %copy-done), channel_id=1, source_target_pairs={{0,12},{4,8},{8,4},{12,0},{1,13},{5,9},{9,5},{13,1},{2,14},{6,10},... | collective-permute-start | bytes 3145736 | tf_op jit(solution)/shard_map/ppermute | solution.py:72
  96.3 60.1 %collective-permute-start.21 = (bf16[512,1024]{1,0:T(8,128)(2,1)S(1)}, bf16[512,1024]{1,0:T(8,128)(2,1)}, u32[]{:S(2)}, u32[]{:S(2)}) collective-permute-start(bf16[512,1024]{1,0:T(8,128)(2,1)S(1)} %copy-done), channel_id=1, source_target_pairs={{0,8},{4,12},{8,0},{12,4},{1,9},{5,13},{9,1},{13,5},{2,10},{6,14},... | collective-permute-start | bytes 3145736 | tf_op jit(solution)/shard_map/ppermute | solution.py:73
  128.7 33.3 %all-to-all-start.2 = ((bf16[16,16,4096]{2,1,0:T(8,128)(2,1)}), bf16[16,16,4096]{2,1,0:T(8,128)(2,1)S(1)}, u32[]{:S(2)}, u32[]{:S(2)}) async-start(bf16[16,16,4096]{2,1,0:T(8,128)(2,1)} %bitcast.189), calls=%async_computation.2 | async-start | bytes 4194304 | tf_op jit(solution)/shard_map/all_to_all | solution.py:209
  132.4 25.6 %collective-permute-start.16 = (bf16[512,1024]{1,0:T(8,128)(2,1)S(1)}, bf16[512,1024]{1,0:T(8,128)(2,1)S(1)}, u32[]{:S(2)}, u32[]{:S(2)}) collective-permute-start(bf16[512,1024]{1,0:T(8,128)(2,1)S(1)} %copy-done), channel_id=1, source_target_pairs={{0,1},{1,0},{2,3},{3,2},{4,5},{5,4},{6,7},{7,6},{8,9},{9,8},{10,11... | collective-permute-start | bytes 3145736 | tf_op jit(solution)/shard_map/ppermute | solution.py:58
  135.3 23.7 %collective-permute-start.18 = (bf16[512,1024]{1,0:T(8,128)(2,1)}, bf16[512,1024]{1,0:T(8,128)(2,1)S(1)}, u32[]{:S(2)}, u32[]{:S(2)}) collective-permute-start(bf16[512,1024]{1,0:T(8,128)(2,1)} %collective-permute-done.17.refs_3_), channel_id=1, source_target_pairs={{0,1},{1,0},{2,3},{3,2},{4,5},{5,4},{6,7},{7,6},{8,9},{9,8},{10,11... | collective-permute-start | bytes 3145736 | tf_op jit(solution)/shard_map/ppermute | solution.py:58
  135.4 24.5 %collective-permute-start.20 = (bf16[512,1024]{1,0:T(8,128)(2,1)}, bf16[512,1024]{1,0:T(8,128)(2,1)S(1)}, u32[]{:S(2)}, u32[]{:S(2)}) collective-permute-start(bf16[512,1024]{1,0:T(8,128)(2,1)} %collective-permute-done.19.refs_5_), channel_id=1, source_target_pairs={{0,1},{1,0},{2,3},{3,2},{4,5},{5,4},{6,7},{7,6},{8,9},{9,8},{10,11... | collective-permute-start | bytes 3145736 | tf_op jit(solution)/shard_map/ppermute | solution.py:58
  156.4 4.6 %collective-permute-start.22 = (bf16[512,1024]{1,0:T(8,128)(2,1)}, bf16[512,1024]{1,0:T(8,128)(2,1)S(1)}, u32[]{:S(2)}, u32[]{:S(2)}) collective-permute-start(bf16[512,1024]{1,0:T(8,128)(2,1)} %collective-permute-done.21.refs_7_), channel_id=1, source_target_pairs={{0,1},{1,0},{2,3},{3,2},{4,5},{5,4},{6,7},{7,6},{8,9},{9,8},{10,11... | collective-permute-start | bytes 3145736 | tf_op jit(solution)/shard_map/ppermute | solution.py:58
  171.7 15.8 %all-to-all-start.3 = ((bf16[8,32,1024]{2,1,0:T(8,128)(2,1)}), bf16[8,32,1024]{2,1,0:T(8,128)(2,1)}, u32[]{:S(2)}, u32[]{:S(2)}) async-start(bf16[8,32,1024]{2,1,0:T(8,128)(2,1)} %shard_map.105), calls=%async_computation.3 | async-start | bytes 1048576 | tf_op jit(solution)/shard_map/all_to_all | solution.py:229
  187.5 11.1 %all-to-all-start.4 = ((bf16[8,32,1024]{2,1,0:T(8,128)(2,1)}), bf16[8,32,1024]{2,1,0:T(8,128)(2,1)S(1)}, u32[]{:S(2)}, u32[]{:S(2)}) async-start(bf16[8,32,1024]{2,1,0:T(8,128)(2,1)} %all-to-all-done.3), calls=%async_computation.4 | async-start | bytes 1048576 | tf_op jit(solution)/shard_map/all_to_all | solution.py:230
  199.6 8.2 %all-to-all-start.5 = ((f32[8,1,128]{2,1,0:T(1,128)}), f32[8,1,128]{2,1,0:T(1,128)S(1)}, u32[]{:S(2)}, u32[]{:S(2)}) async-start(f32[8,1,128]{2,1,0:T(1,128)} %broadcast_in_dim.25), calls=%async_computation.5 | async-start | bytes 8192 | tf_op jit(solution)/shard_map/all_to_all | solution.py:234
  210.1 5.9 %collective-permute-start.24 = (bf16[2,128,512]{2,1,0:T(8,128)(2,1)S(1)}, bf16[2,128,512]{2,1,0:T(8,128)(2,1)S(1)}, u32[]{:S(2)}, u32[]{:S(2)}) collective-permute-start(bf16[2,128,512]{2,1,0:T(8,128)(2,1)S(1)} %bitcast.201), channel_id=1, source_target_pairs={{0,1},{1,0},{2,3},{3,2},{4,5},{5,4},{6,7},{7,6},{8,9},{9,8},{10,11... | collective-permute-start | bytes 786440 | tf_op jit(solution)/shard_map/ppermute | solution.py:58
  (28 other events, 110.3 us)

commit v2 on v1

--- a/solution.py
+++ b/solution.py
@@ -58,14 +58,23 @@
     return lax.ppermute(v, axis, FLIP)
 
 
-def cube_of(w):
-    half = w.shape[0] // 2
-    far_z, far_y = swap(w, "zl"), swap(w, "yl")
-    top, bottom = swap(far_z[:half], "yl"), swap(far_y[half:], "zl")
-    pieces = []
-    for dz, dy, row, v in ((0, 0, 0, w), (1, 0, 0, far_z), (0, 1, 0, far_y), (1, 1, 0, top), (1, 1, half, bottom)):
-        pieces += [(dz, dy, 0, row, v), (dz, dy, 1, row, swap(v, "c"))]
-    return pieces
+def cube_of(top, bottom):
+    z_top, y_bottom = swap(top, "zl"), swap(bottom, "yl")
+    z_bottom, y_top = swap(bottom, "zl"), swap(top, "yl")
+    d_bottom, d_top = swap(y_bottom, "zl"), swap(z_top, "yl")
+    near, far = [], []
+    for pieces, dz, half, v in (
+        (near, 0, 0, top),
+        (near, 0, 1, bottom),
+        (near, 1, 0, z_top),
+        (near, 1, 1, z_bottom),
+        (far, 0, 1, y_bottom),
+        (far, 0, 0, y_top),
+        (far, 1, 0, d_top),
+        (far, 1, 1, d_bottom),
+    ):
+        pieces += [(dz, 0, half, v), (dz, 1, half, swap(v, "c"))]
+    return near, far
 
 
 def row_of(w):
@@ -122,7 +131,7 @@
         + [pltpu.SemaphoreType.DMA((n,))],
         compiler_params=pltpu.CompilerParams(vmem_limit_bytes=30 << 20),
         cost_estimate=pl.CostEstimate(flops=flops, bytes_accessed=sum(2 * w.size for _, _, w in weights), transcendentals=0),
-    )(jnp.stack(scalars).astype(jnp.int32), *lhs_pieces, *[w for _, _, w in weights])
+    )(jnp.stack(scalars).astype(jnp.int32), *lhs_pieces, *[pltpu.with_memory_space_constraint(w, pltpu.HBM) for _, _, w in weights])
 
 
 def unrelated(pieces, index):
@@ -151,7 +160,8 @@
 
     q_cols = w_query.shape[1]
     rows, cols = w_query.shape[0], q_cols + w_keyval.shape[1]
-    w_qkv = cube_of(jnp.concatenate([w_query, w_keyval], axis=1))
+    halves = [jnp.concatenate([w_query[i : i + rows // 2], w_keyval[i : i + rows // 2]], axis=1) for i in (0, rows // 2)]
+    w_near, w_far = cube_of(*halves)
     w_out = row_of(w_output)
 
     sent = h.reshape(4, 4, seq_dev, width).transpose(1, 0, 2, 3).reshape(4, quarter, width)
@@ -181,19 +191,25 @@
     def put_columns(scalar_ref, out_ref, slot, value):
         out_ref[:, slot * cols : (slot + 1) * cols] = value
 
-    partial = matmul_kernel(
-        slots,
-        [(dz * rows + row, dy * 2 + dc, v) for dz, dy, dc, row, v in w_qkv],
-        (tokens, 4 * cols),
-        place_tokens,
-        put_columns,
-        [order],
-    ).reshape(16, seq_dev, 4 * cols)
-    arrived = lax.all_to_all(partial, WIDE, 0, 0, tiled=True)
-    qkv = jnp.sum(arrived.reshape(4, 4, seq_dev, 4 * cols).astype(F32), axis=0)
+    arrived = []
+    for pieces in (w_near, w_far):
+        partial = matmul_kernel(
+            slots,
+            [(dz * rows + half * (rows // 2), dc, v) for dz, dc, half, v in pieces],
+            (tokens, 2 * cols),
+            place_tokens,
+            put_columns,
+            [order],
+        ).reshape(16, seq_dev, 2 * cols)
+        arrived.append(lax.all_to_all(partial, WIDE, 0, 0, tiled=True))
+    qkv = [jnp.sum(v.reshape(4, 4, seq_dev, 2 * cols).astype(F32), axis=0) for v in arrived]
     pair_pos = lax.axis_index(PAIR)
-    q_of = [unrelated([qkv[x, :, p * cols : p * cols + q_cols] for p in range(4)], pair_pos) for x in range(4)]
-    kv_of = [unrelated([qkv[x, :, p * cols + q_cols : (p + 1) * cols] for p in range(4)], pair_pos) for x in range(4)]
+
+    def head_block(x, p, start, stop):
+        return qkv[p // 2][x, :, (p % 2) * cols + start : (p % 2) * cols + stop]
+
+    q_of = [unrelated([head_block(x, p, 0, q_cols) for p in range(4)], pair_pos) for x in range(4)]
+    kv_of = [unrelated([head_block(x, p, q_cols, cols) for p in range(4)], pair_pos) for x in range(4)]
     queries = jnp.concatenate([v for x in q_of for v in x], axis=1).reshape(seq_dev, -1, head_dim)
     keyval = jnp.concatenate([v for x in kv_of for v in x], axis=1).reshape(seq_dev, -1, head_dim)
     own_len = lax.dynamic_slice_in_dim(lengths, shard * seq_dev, seq_dev)
@@ -238,9 +254,10 @@
     both = jnp.stack([summed.astype(BF16), ffn_input]).reshape(2, tokens // 2, 2, width)
     keep = lax.dynamic_index_in_dim(both, core, 2, keepdims=False)
     came = swap(lax.dynamic_index_in_dim(both, 1 - core, 2, keepdims=False), "c")
-    both = unrelated([v.reshape(2, 8, seq_dev, width) for v in (keep, came)], core)
-    both = jnp.stack(both, axis=2).reshape(2, tokens, width)
-    return both[0], both[1]
+    keep, came = keep.reshape(2, 8, seq_dev, width), came.reshape(2, 8, seq_dev, width)
+    return tuple(
+        jnp.stack(unrelated([keep[i], came[i]], core), axis=1).reshape(tokens, width) for i in range(2)
+    )
 
 
 def solution(mesh):

time: 219 us -> 261 us (1.19)
  waiting for transfers between devices: 71.4 us -> 130 us
  local copies, waits for them, and re-layouts: 22.8 us -> 11.1 us
  starting transfers between devices: 95.9 us -> 86.7 us
  Pallas kernels: 11.4 us -> 16 us
    all_to_all x1 -> x2, waiting for transfers between devices: 18.4 us -> 53.5 us  [local(): arrived.append(lax.all_to_all(partial, WIDE, 0, 0, tiled=True))]
    ppermute x1, waiting for transfers between devices: 20.6 us -> 0.01 us  [row_of(): near[2] = lax.ppermute(w, 'x', xor_pairs(2))]
    all_to_all x1, waiting for transfers between devices: 0.01 us -> 20.6 us  [local(): lax.all_to_all(context, ACROSS, 0, 0, tiled=True).reshape(tokens, 2 * wide)]
    ppermute x15 -> x20, waiting for transfers between devices: 7.87 us -> 23.2 us  [swap(): return lax.ppermute(v, axis, FLIP)]
    unnamed x45 -> x33, local copies, waits for them, and re-layouts: 14 us -> 1.85 us
    ppermute x3, waiting for transfers between devices: 3.64 us -> 11.7 us  [local(): lax.ppermute(normed, 'x', xor_pairs(k))]
    ppermute x3, starting transfers between devices: 26.5 us -> 18.6 us  [local(): lax.ppermute(normed, 'x', xor_pairs(k))]
    pallas_call x2 -> x3, Pallas kernels: 11.4 us -> 16 us  [matmul_kernel(): pl.pallas_call(body, out_shape=jax.ShapeDtypeStruct(out_shape, BF16), in_...]
  transfers between devices with their start and end apart: 31 -> 37, of which waited for: 14 -> 19; matrix products, arithmetic and copies ran while one was open for 8% -> 7% of each run, Pallas kernels for 0% -> 4%
where the time goes in v2:
time: 261 us; the launch traced here: 260 us
  waiting for transfers between devices  130 us (50%)
  starting transfers between devices  86.7 us (33%)
  Pallas kernels  16 us (6%)
  local copies, waits for them, and re-layouts  11.1 us (4%)
  matrix products  8.73 us (3%)
  other arithmetic  6.21 us (2%)
    all_to_all x2, waiting for transfers between devices, local(): arrived.append(lax.all_to_all(partial, WIDE, 0, 0, tiled=True))  53.5 us
    ppermute x20, starting transfers between devices, swap(): return lax.ppermute(v, axis, FLIP)  27.5 us
    ppermute x20, waiting for transfers between devices, swap(): return lax.ppermute(v, axis, FLIP)  23.2 us
    all_to_all x1, waiting for transfers between devices, local(): lax.all_to_all(context, ACROSS, 0, 0, tiled=True).reshape(tokens, 2 * wide)  20.6 us
    ppermute x3, starting transfers between devices, local(): lax.ppermute(normed, 'x', xor_pairs(k))  18.6 us
    pallas_call x3, Pallas kernels, matmul_kernel(): pl.pallas_call(body, out_shape=jax.ShapeDtypeStruct(out_shape, BF16), in_...  16 us
    ppermute x3, waiting for transfers between devices, local(): lax.ppermute(normed, 'x', xor_pairs(k))  11.7 us
    all_to_all x2, starting transfers between devices, local(): arrived.append(lax.all_to_all(partial, WIDE, 0, 0, tiled=True))  10 us
  transfers between devices with their start and end apart: 37, of which 19 were waited for; matrix products, arithmetic and copies ran while one was open for 7% of the time, Pallas kernels for 4%

profile of v2, /device:TPU:1, one launch (start us, length us, event | category | flops | bytes accessed | tf_op | source)
XLA Modules:
  0.0 259.9 jit_solution(16191668651653732906)
XLA Ops:
  2.4 4.8 %all-to-all-start = ((bf16[4,64,512]{2,1,0:T(8,128)(2,1)}), bf16[4,64,512]{2,1,0:T(8,128)(2,1)S(1)}, u32[]{:S(2)}, u32[]{:S(2)}) async-start(bf16[4,64,512]{2,1,0:T(8,128)(2,1)} %bitcast.5), calls=%async_computation | async-start | bytes 524288 | tf_op jit(solution)/shard_map/all_to_all | solution.py:168
  27.6 7.0 %collective-permute-done.7.refs_4_ = bf16[512,640]{1,0:T(8,128)(2,1)} collective-permute-done((bf16[512,640]{1,0:T(8,128)(2,1)S(1)}, bf16[512,640]{1,0:T(8,128)(2,1)}, u32[]{:S(2)}, u32[]{:S(2)}) %collective-permute-start.7) | collective-permute-done | bytes 655392 | tf_op jit(solution)/shard_map/ppermute | solution.py:58
  34.5 3.9 %collective-permute-start.4 = (bf16[64,2048]{1,0:T(8,128)(2,1)S(1)}, bf16[64,2048]{1,0:T(8,128)(2,1)S(1)}, u32[]{:S(2)}, u32[]{:S(2)}) collective-permute-start(bf16[64,2048]{1,0:T(8,128)(2,1)S(1)} %collective-permute-done.3.refs_0_), channel_id=1, source_target_pairs={{0,4},{4,0},{8,12},{12,8},{1,5},{5,1},{9,13},{13,9},{2,6},{6,2},{1... | collective-permute-start | bytes 786440 | tf_op jit(solution)/shard_map/ppermute | solution.py:182
  38.4 10.2 %collective-permute-done.9.refs_6_ = bf16[512,640]{1,0:T(8,128)(2,1)} collective-permute-done((bf16[512,640]{1,0:T(8,128)(2,1)S(1)}, bf16[512,640]{1,0:T(8,128)(2,1)}, u32[]{:S(2)}, u32[]{:S(2)}) %collective-permute-start.9) | collective-permute-done | bytes 655392 | tf_op jit(solution)/shard_map/ppermute | solution.py:58
  51.1 3.7 %collective-permute-start.18 = (bf16[512,640]{1,0:T(8,128)(2,1)S(1)}, bf16[512,640]{1,0:T(8,128)(2,1)S(1)}, u32[]{:S(2)}, u32[]{:S(2)}) collective-permute-start(bf16[512,640]{1,0:T(8,128)(2,1)S(1)} %collective-permute-done.11.refs_8_), channel_id=1, source_target_pairs={{0,1},{1,0},{2,3},{3,2},{4,5},{5,4},{6,7},{7,6},{8,9},{9,8},{10,11... | collective-permute-start | bytes 1966088 | tf_op jit(solution)/shard_map/ppermute | solution.py:58
  54.9 9.4 %collective-permute-start.5 = (bf16[64,2048]{1,0:T(8,128)(2,1)S(1)}, bf16[64,2048]{1,0:T(8,128)(2,1)S(1)}, u32[]{:S(2)}, u32[]{:S(2)}) collective-permute-start(bf16[64,2048]{1,0:T(8,128)(2,1)S(1)} %collective-permute-done.3.refs_0_), channel_id=1, source_target_pairs={{0,8},{4,12},{8,0},{12,4},{1,9},{5,13},{9,1},{13,5},{2,10},{6,14},... | collective-permute-start | bytes 786440 | tf_op jit(solution)/shard_map/ppermute | solution.py:182
  64.4 6.3 %collective-permute-done.5.refs_2_ = bf16[64,2048]{1,0:T(8,128)(2,1)S(1)} collective-permute-done((bf16[64,2048]{1,0:T(8,128)(2,1)S(1)}, bf16[64,2048]{1,0:T(8,128)(2,1)S(1)}, u32[]{:S(2)}, u32[]{:S(2)}) %collective-permute-start.5) | collective-permute-done | bytes 262176 | tf_op jit(solution)/shard_map/ppermute | solution.py:182
  70.6 5.3 %collective-permute-start.6 = (bf16[64,2048]{1,0:T(8,128)(2,1)S(1)}, bf16[64,2048]{1,0:T(8,128)(2,1)S(1)}, u32[]{:S(2)}, u32[]{:S(2)}) collective-permute-start(bf16[64,2048]{1,0:T(8,128)(2,1)S(1)} %collective-permute-done.3.refs_0_), channel_id=1, source_target_pairs={{0,12},{4,8},{8,4},{12,0},{1,13},{5,9},{9,5},{13,1},{2,14},{6,10},... | collective-permute-start | bytes 786440 | tf_op jit(solution)/shard_map/ppermute | solution.py:182
  75.9 5.4 %collective-permute-done.6.refs_3_ = bf16[64,2048]{1,0:T(8,128)(2,1)S(1)} collective-permute-done((bf16[64,2048]{1,0:T(8,128)(2,1)S(1)}, bf16[64,2048]{1,0:T(8,128)(2,1)S(1)}, u32[]{:S(2)}, u32[]{:S(2)}) %collective-permute-start.6) | collective-permute-done | bytes 262176 | tf_op jit(solution)/shard_map/ppermute | solution.py:182
  84.5 5.3 %shard_map.105 = bf16[256,1280]{1,0:T(8,128)(2,1)} custom-call(s32[1]{0:T(128)} %bitcast.2.scalar_ref, bf16[64,2048]{1,0:T(8,128)(2,1)S(1)} %collective-permute-done.3.refs_0_, bf16[64,2048]{1,0:T(8,128)(2,1)S(1)} %collective-permute-done.4.refs_1_, bf16[64,2048]{1,0:T(8,128)(2,1)S(1)} %collective-permute-done.5.refs_2_, ...), custom_call_target="tpu_custom_call" | custom-call | flops 1342177280 | bytes 5242880 | tf_op jit(solution)/shard_map/pallas_call | solution.py:122
  89.8 6.3 %all-to-all-start.2 = ((bf16[16,16,1280]{2,1,0:T(8,128)(2,1)}), bf16[16,16,1280]{2,1,0:T(8,128)(2,1)S(1)}, u32[]{:S(2)}, u32[]{:S(2)}) async-start(bf16[16,16,1280]{2,1,0:T(8,128)(2,1)} %bitcast.9), calls=%async_computation.2 | async-start | bytes 1310720 | tf_op jit(solution)/shard_map/all_to_all | solution.py:204
  100.3 5.1 %shard_map.104 = bf16[256,1280]{1,0:T(8,128)(2,1)} custom-call(s32[1]{0:T(128)} %bitcast.2.scalar_ref, bf16[64,2048]{1,0:T(8,128)(2,1)S(1)} %collective-permute-done.3.refs_0_, bf16[64,2048]{1,0:T(8,128)(2,1)S(1)} %collective-permute-done.4.refs_1_, bf16[64,2048]{1,0:T(8,128)(2,1)S(1)} %collective-permute-done.5.refs_2_, ...), custom_call_target="tpu_custom_call" | custom-call | flops 1342177280 | bytes 5242880 | tf_op jit(solution)/shard_map/pallas_call | solution.py:122
  105.5 5.7 %all-to-all-done.2 = bf16[16,16,1280]{2,1,0:T(8,128)(2,1)S(1)} async-done(((bf16[16,16,1280]{2,1,0:T(8,128)(2,1)}), bf16[16,16,1280]{2,1,0:T(8,128)(2,1)S(1)}, u32[]{:S(2)}, u32[]{:S(2)}) %all-to-all-start.2) | async-done | bytes 655392 | tf_op jit(solution)/shard_map/all_to_all | solution.py:204
  111.2 3.8 %all-to-all-start.1 = ((bf16[16,16,1280]{2,1,0:T(8,128)(2,1)}), bf16[16,16,1280]{2,1,0:T(8,128)(2,1)S(1)}, u32[]{:S(2)}, u32[]{:S(2)}) async-start(bf16[16,16,1280]{2,1,0:T(8,128)(2,1)} %bitcast.7), calls=%async_computation.1 | async-start | bytes 1310720 | tf_op jit(solution)/shard_map/all_to_all | solution.py:204
  115.3 47.8 %all-to-all-done.1 = bf16[16,16,1280]{2,1,0:T(8,128)(2,1)S(1)} async-done(((bf16[16,16,1280]{2,1,0:T(8,128)(2,1)}), bf16[16,16,1280]{2,1,0:T(8,128)(2,1)S(1)}, u32[]{:S(2)}, u32[]{:S(2)}) %all-to-all-start.1) | async-done | bytes 655392 | tf_op jit(solution)/shard_map/all_to_all | solution.py:204
  165.0 6.6 %fusion.32 = (f32[16,8,8]{2,1,0:T(8,128)S(1)}, f32[16,8,8,192]{3,2,1,0:T(8,128)S(1)}) fusion(bf16[16,8,192,128]{3,2,1,0:T(8,128)(2,1)} %param.15, bf16[16,8,8,64]{3,2,1,0:T(8,128)(2,1)S(1)} %get-tuple-element.7, bf16[16,8,8,64]{3,2,1,0:T(8,128)(2,1)S(1)} %get-tuple-element.6, pred[16,192]{1,0:T(8,128)(4,1)S(1)} %iota_compare_fusion), kind=kOutput, calls=%fused_computation.139 | convolution fusion | flops 51444736 | bytes 7347200 | tf_op jit(solution)/shard_map/nkgd,nkld->nkgl/dot_general | solution.py:31
  175.9 3.7 %all-to-all-start.3 = ((bf16[16,16,4096]{2,1,0:T(8,128)(2,1)}), bf16[16,16,4096]{2,1,0:T(8,128)(2,1)S(1)}, u32[]{:S(2)}, u32[]{:S(2)}) async-start(bf16[16,16,4096]{2,1,0:T(8,128)(2,1)} %bitcast.194), calls=%async_computation.3 | async-start | bytes 4194304 | tf_op jit(solution)/shard_map/all_to_all | solution.py:225
  188.1 20.6 %all-to-all-done.3 = bf16[16,16,4096]{2,1,0:T(8,128)(2,1)S(1)} async-done(((bf16[16,16,4096]{2,1,0:T(8,128)(2,1)}), bf16[16,16,4096]{2,1,0:T(8,128)(2,1)S(1)}, u32[]{:S(2)}, u32[]{:S(2)}) %all-to-all-start.3) | async-done | bytes 2097184 | tf_op jit(solution)/shard_map/all_to_all | solution.py:225
  208.7 5.6 %shard_map.106 = bf16[8,32,1024]{2,1,0:T(8,128)(2,1)} custom-call(s32[2]{0:T(128)S(1)} %pad_add_fusion.scalar_ref, bf16[256,4096]{1,0:T(8,128)(2,1)S(1)} %bitcast.193, bf16[512,1024]{1,0:T(8,128)(2,1)} %refs_1_.1, bf16[512,1024]{1,0:T(8,128)(2,1)} %copy-done.4, bf16[512,1024]{1,0:T(8,128)(2,1)} %collective-permute-done.22.refs_3_, ...), custom_call_target="tpu_custom_call" | custom-call | flops 2147483648 | bytes 8388608 | tf_op jit(solution)/shard_map/pallas_call | solution.py:122
  214.4 6.4 %all-to-all-start.4 = ((bf16[8,32,1024]{2,1,0:T(8,128)(2,1)}), bf16[8,32,1024]{2,1,0:T(8,128)(2,1)}, u32[]{:S(2)}, u32[]{:S(2)}) async-start(bf16[8,32,1024]{2,1,0:T(8,128)(2,1)} %shard_map.106), calls=%async_computation.4 | async-start | bytes 1048576 | tf_op jit(solution)/shard_map/all_to_all | solution.py:245
  220.8 9.3 %all-to-all-done.4 = bf16[8,32,1024]{2,1,0:T(8,128)(2,1)} async-done(((bf16[8,32,1024]{2,1,0:T(8,128)(2,1)}), bf16[8,32,1024]{2,1,0:T(8,128)(2,1)}, u32[]{:S(2)}, u32[]{:S(2)}) %all-to-all-start.4) | async-done | bytes 524320 | tf_op jit(solution)/shard_map/all_to_all | solution.py:245
  241.5 3.5 %all-to-all-start.6 = ((f32[8,1,128]{2,1,0:T(1,128)}), f32[8,1,128]{2,1,0:T(1,128)S(1)}, u32[]{:S(2)}, u32[]{:S(2)}) async-start(f32[8,1,128]{2,1,0:T(1,128)} %broadcast_in_dim.25), calls=%async_computation.6 | async-start | bytes 8192 | tf_op jit(solution)/shard_map/all_to_all | solution.py:250
  246.0 3.7 %all-to-all-done.6 = f32[8,1,128]{2,1,0:T(1,128)S(1)} async-done(((f32[8,1,128]{2,1,0:T(1,128)}), f32[8,1,128]{2,1,0:T(1,128)S(1)}, u32[]{:S(2)}, u32[]{:S(2)}) %all-to-all-start.6) | async-done | bytes 4128 | tf_op jit(solution)/shard_map/all_to_all | solution.py:250
  252.1 5.0 %collective-permute-start.29 = (bf16[2,128,512]{2,1,0:T(8,128)(2,1)S(1)}, bf16[2,128,512]{2,1,0:T(8,128)(2,1)S(1)}, u32[]{:S(2)}, u32[]{:S(2)}) collective-permute-start(bf16[2,128,512]{2,1,0:T(8,128)(2,1)S(1)} %bitcast.210), channel_id=1, source_target_pairs={{0,1},{1,0},{2,3},{3,2},{4,5},{5,4},{6,7},{7,6},{8,9},{9,8},{10,11... | collective-permute-start | bytes 786440 | tf_op jit(solution)/shard_map/ppermute | solution.py:58
  (178 shorter events, 64.1 us)
Async XLA Ops:
  8.5 19.0 %collective-permute-start.11 = (bf16[512,640]{1,0:T(8,128)(2,1)S(1)}, bf16[512,640]{1,0:T(8,128)(2,1)S(1)}, u32[]{:S(2)}, u32[]{:S(2)}) collective-permute-start(bf16[512,640]{1,0:T(8,128)(2,1)S(1)} %pad_maximum_fusion.1.refs_4_), channel_id=1, source_target_pairs={{0,16},{16,0},{1,17},{17,1},{2,18},{18,2},{3,19},{19,3},{4,20},{20... | collective-permute-start | bytes 1966088 | tf_op jit(solution)/shard_map/ppermute | solution.py:58
  20.7 13.8 %collective-permute-start.7 = (bf16[512,640]{1,0:T(8,128)(2,1)S(1)}, bf16[512,640]{1,0:T(8,128)(2,1)}, u32[]{:S(2)}, u32[]{:S(2)}) collective-permute-start(bf16[512,640]{1,0:T(8,128)(2,1)S(1)} %pad_maximum_fusion.refs_6_), channel_id=1, source_target_pairs={{0,2},{2,0},{1,3},{3,1},{4,6},{6,4},{5,7},{7,5},{8,10},{10,8},{9,1... | collective-permute-start | bytes 1966088 | tf_op jit(solution)/shard_map/ppermute | solution.py:58
  21.3 27.3 %collective-permute-start.9 = (bf16[512,640]{1,0:T(8,128)(2,1)S(1)}, bf16[512,640]{1,0:T(8,128)(2,1)}, u32[]{:S(2)}, u32[]{:S(2)}) collective-permute-start(bf16[512,640]{1,0:T(8,128)(2,1)S(1)} %pad_maximum_fusion.1.refs_4_), channel_id=1, source_target_pairs={{0,2},{2,0},{1,3},{3,1},{4,6},{6,4},{5,7},{7,5},{8,10},{10,8},{9,1... | collective-permute-start | bytes 1966088 | tf_op jit(solution)/shard_map/ppermute | solution.py:58
  22.3 27.1 %collective-permute-start.19 = (bf16[512,640]{1,0:T(8,128)(2,1)S(1)}, bf16[512,640]{1,0:T(8,128)(2,1)}, u32[]{:S(2)}, u32[]{:S(2)}) collective-permute-start(bf16[512,640]{1,0:T(8,128)(2,1)S(1)} %pad_maximum_fusion.refs_6_), channel_id=1, source_target_pairs={{0,16},{16,0},{1,17},{17,1},{2,18},{18,2},{3,19},{19,3},{4,20},{20... | collective-permute-start | bytes 1966088 | tf_op jit(solution)/shard_map/ppermute | solution.py:58
  23.9 27.1 %collective-permute-start.16 = (bf16[512,640]{1,0:T(8,128)(2,1)S(1)}, bf16[512,640]{1,0:T(8,128)(2,1)S(1)}, u32[]{:S(2)}, u32[]{:S(2)}) collective-permute-start(bf16[512,640]{1,0:T(8,128)(2,1)S(1)} %pad_maximum_fusion.1.refs_4_), channel_id=1, source_target_pairs={{0,1},{1,0},{2,3},{3,2},{4,5},{5,4},{6,7},{7,6},{8,9},{9,8},{10,11... | collective-permute-start | bytes 1966088 | tf_op jit(solution)/shard_map/ppermute | solution.py:58
  27.5 27.3 %collective-permute-start.17 = (bf16[512,640]{1,0:T(8,128)(2,1)S(1)}, bf16[512,640]{1,0:T(8,128)(2,1)S(1)}, u32[]{:S(2)}, u32[]{:S(2)}) collective-permute-start(bf16[512,640]{1,0:T(8,128)(2,1)S(1)} %pad_maximum_fusion.refs_6_), channel_id=1, source_target_pairs={{0,1},{1,0},{2,3},{3,2},{4,5},{5,4},{6,7},{7,6},{8,9},{9,8},{10,11... | collective-permute-start | bytes 1966088 | tf_op jit(solution)/shard_map/ppermute | solution.py:58
  34.5 20.4 %collective-permute-start.4 = (bf16[64,2048]{1,0:T(8,128)(2,1)S(1)}, bf16[64,2048]{1,0:T(8,128)(2,1)S(1)}, u32[]{:S(2)}, u32[]{:S(2)}) collective-permute-start(bf16[64,2048]{1,0:T(8,128)(2,1)S(1)} %collective-permute-done.3.refs_0_), channel_id=1, source_target_pairs={{0,4},{4,0},{8,12},{12,8},{1,5},{5,1},{9,13},{13,9},{2,6},{6,2},{1... | collective-permute-start | bytes 786440 | tf_op jit(solution)/shard_map/ppermute | solution.py:182
  48.6 34.6 %collective-permute-start.12 = (bf16[512,640]{1,0:T(8,128)(2,1)S(1)}, bf16[512,640]{1,0:T(8,128)(2,1)}, u32[]{:S(2)}, u32[]{:S(2)}) collective-permute-start(bf16[512,640]{1,0:T(8,128)(2,1)S(1)} %collective-permute-done.11.refs_8_), channel_id=1, source_target_pairs={{0,2},{2,0},{1,3},{3,1},{4,6},{6,4},{5,7},{7,5},{8,10},{10,8},{9,1... | collective-permute-start | bytes 1966088 | tf_op jit(solution)/shard_map/ppermute | solution.py:58
  49.4 33.8 %collective-permute-start.14 = (bf16[512,640]{1,0:T(8,128)(2,1)}, bf16[512,640]{1,0:T(8,128)(2,1)}, u32[]{:S(2)}, u32[]{:S(2)}) collective-permute-start(bf16[512,640]{1,0:T(8,128)(2,1)} %collective-permute-done.7.refs_4_), channel_id=1, source_target_pairs={{0,16},{16,0},{1,17},{17,1},{2,18},{18,2},{3,19},{19,3},{4,20},{20... | collective-permute-start | bytes 1966088 | tf_op jit(solution)/shard_map/ppermute | solution.py:58
  51.1 32.6 %collective-permute-start.18 = (bf16[512,640]{1,0:T(8,128)(2,1)S(1)}, bf16[512,640]{1,0:T(8,128)(2,1)S(1)}, u32[]{:S(2)}, u32[]{:S(2)}) collective-permute-start(bf16[512,640]{1,0:T(8,128)(2,1)S(1)} %collective-permute-done.11.refs_8_), channel_id=1, source_target_pairs={{0,1},{1,0},{2,3},{3,2},{4,5},{5,4},{6,7},{7,6},{8,9},{9,8},{10,11... | collective-permute-start | bytes 1966088 | tf_op jit(solution)/shard_map/ppermute | solution.py:58
  54.8 29.1 %collective-permute-start.20 = (bf16[512,640]{1,0:T(8,128)(2,1)}, bf16[512,640]{1,0:T(8,128)(2,1)}, u32[]{:S(2)}, u32[]{:S(2)}) collective-permute-start(bf16[512,640]{1,0:T(8,128)(2,1)} %collective-permute-done.19.refs_10_), channel_id=1, source_target_pairs={{0,1},{1,0},{2,3},{3,2},{4,5},{5,4},{6,7},{7,6},{8,9},{9,8},{10,11... | collective-permute-start | bytes 1966088 | tf_op jit(solution)/shard_map/ppermute | solution.py:58
  54.9 15.7 %collective-permute-start.5 = (bf16[64,2048]{1,0:T(8,128)(2,1)S(1)}, bf16[64,2048]{1,0:T(8,128)(2,1)S(1)}, u32[]{:S(2)}, u32[]{:S(2)}) collective-permute-start(bf16[64,2048]{1,0:T(8,128)(2,1)S(1)} %collective-permute-done.3.refs_0_), channel_id=1, source_target_pairs={{0,8},{4,12},{8,0},{12,4},{1,9},{5,13},{9,1},{13,5},{2,10},{6,14},... | collective-permute-start | bytes 786440 | tf_op jit(solution)/shard_map/ppermute | solution.py:182
  70.6 10.7 %collective-permute-start.6 = (bf16[64,2048]{1,0:T(8,128)(2,1)S(1)}, bf16[64,2048]{1,0:T(8,128)(2,1)S(1)}, u32[]{:S(2)}, u32[]{:S(2)}) collective-permute-start(bf16[64,2048]{1,0:T(8,128)(2,1)S(1)} %collective-permute-done.3.refs_0_), channel_id=1, source_target_pairs={{0,12},{4,8},{8,4},{12,0},{1,13},{5,9},{9,5},{13,1},{2,14},{6,10},... | collective-permute-start | bytes 786440 | tf_op jit(solution)/shard_map/ppermute | solution.py:182
  81.3 16.4 %collective-permute-start.8 = (bf16[512,640]{1,0:T(8,128)(2,1)}, bf16[512,640]{1,0:T(8,128)(2,1)}, u32[]{:S(2)}, u32[]{:S(2)}) collective-permute-start(bf16[512,640]{1,0:T(8,128)(2,1)} %collective-permute-done.7.refs_4_), channel_id=1, source_target_pairs={{0,1},{1,0},{2,3},{3,2},{4,5},{5,4},{6,7},{7,6},{8,9},{9,8},{10,11... | collective-permute-start | bytes 1966088 | tf_op jit(solution)/shard_map/ppermute | solution.py:58
  83.2 16.5 %collective-permute-start.10 = (bf16[512,640]{1,0:T(8,128)(2,1)}, bf16[512,640]{1,0:T(8,128)(2,1)}, u32[]{:S(2)}, u32[]{:S(2)}) collective-permute-start(bf16[512,640]{1,0:T(8,128)(2,1)} %collective-permute-done.9.refs_6_), channel_id=1, source_target_pairs={{0,1},{1,0},{2,3},{3,2},{4,5},{5,4},{6,7},{7,6},{8,9},{9,8},{10,11... | collective-permute-start | bytes 1966088 | tf_op jit(solution)/shard_map/ppermute | solution.py:58
  83.2 17.2 %collective-permute-start.13 = (bf16[512,640]{1,0:T(8,128)(2,1)}, bf16[512,640]{1,0:T(8,128)(2,1)}, u32[]{:S(2)}, u32[]{:S(2)}) collective-permute-start(bf16[512,640]{1,0:T(8,128)(2,1)} %collective-permute-done.12.refs_8_), channel_id=1, source_target_pairs={{0,1},{1,0},{2,3},{3,2},{4,5},{5,4},{6,7},{7,6},{8,9},{9,8},{10,11... | collective-permute-start | bytes 1966088 | tf_op jit(solution)/shard_map/ppermute | solution.py:58
  83.7 16.6 %collective-permute-start.15 = (bf16[512,640]{1,0:T(8,128)(2,1)}, bf16[512,640]{1,0:T(8,128)(2,1)}, u32[]{:S(2)}, u32[]{:S(2)}) collective-permute-start(bf16[512,640]{1,0:T(8,128)(2,1)} %collective-permute-done.14.refs_10_), channel_id=1, source_target_pairs={{0,1},{1,0},{2,3},{3,2},{4,5},{5,4},{6,7},{7,6},{8,9},{9,8},{10,11... | collective-permute-start | bytes 1966088 | tf_op jit(solution)/shard_map/ppermute | solution.py:58
  89.8 21.4 %all-to-all-start.2 = ((bf16[16,16,1280]{2,1,0:T(8,128)(2,1)}), bf16[16,16,1280]{2,1,0:T(8,128)(2,1)S(1)}, u32[]{:S(2)}, u32[]{:S(2)}) async-start(bf16[16,16,1280]{2,1,0:T(8,128)(2,1)} %bitcast.9), calls=%async_computation.2 | async-start | bytes 1310720 | tf_op jit(solution)/shard_map/all_to_all | solution.py:204
  96.1 85.1 %collective-permute-start.22 = (bf16[512,1024]{1,0:T(8,128)(2,1)S(1)}, bf16[512,1024]{1,0:T(8,128)(2,1)}, u32[]{:S(2)}, u32[]{:S(2)}) collective-permute-start(bf16[512,1024]{1,0:T(8,128)(2,1)S(1)} %copy-done.3), channel_id=1, source_target_pairs={{0,4},{4,0},{8,12},{12,8},{1,5},{5,1},{9,13},{13,9},{2,6},{6,2},{1... | collective-permute-start | bytes 3145736 | tf_op jit(solution)/shard_map/ppermute | solution.py:81
  97.8 83.6 %collective-permute-start.24 = (bf16[512,1024]{1,0:T(8,128)(2,1)S(1)}, bf16[512,1024]{1,0:T(8,128)(2,1)}, u32[]{:S(2)}, u32[]{:S(2)}) collective-permute-start(bf16[512,1024]{1,0:T(8,128)(2,1)S(1)} %copy-done.3), channel_id=1, source_target_pairs={{0,12},{4,8},{8,4},{12,0},{1,13},{5,9},{9,5},{13,1},{2,14},{6,10},... | collective-permute-start | bytes 3145736 | tf_op jit(solution)/shard_map/ppermute | solution.py:81
  99.6 82.1 %collective-permute-start.26 = (bf16[512,1024]{1,0:T(8,128)(2,1)S(1)}, bf16[512,1024]{1,0:T(8,128)(2,1)}, u32[]{:S(2)}, u32[]{:S(2)}) collective-permute-start(bf16[512,1024]{1,0:T(8,128)(2,1)S(1)} %copy-done.3), channel_id=1, source_target_pairs={{0,8},{4,12},{8,0},{12,4},{1,9},{5,13},{9,1},{13,5},{2,10},{6,14},... | collective-permute-start | bytes 3145736 | tf_op jit(solution)/shard_map/ppermute | solution.py:82
  111.2 52.0 %all-to-all-start.1 = ((bf16[16,16,1280]{2,1,0:T(8,128)(2,1)}), bf16[16,16,1280]{2,1,0:T(8,128)(2,1)S(1)}, u32[]{:S(2)}, u32[]{:S(2)}) async-start(bf16[16,16,1280]{2,1,0:T(8,128)(2,1)} %bitcast.7), calls=%async_computation.1 | async-start | bytes 1310720 | tf_op jit(solution)/shard_map/all_to_all | solution.py:204
  175.9 32.8 %all-to-all-start.3 = ((bf16[16,16,4096]{2,1,0:T(8,128)(2,1)}), bf16[16,16,4096]{2,1,0:T(8,128)(2,1)S(1)}, u32[]{:S(2)}, u32[]{:S(2)}) async-start(bf16[16,16,4096]{2,1,0:T(8,128)(2,1)} %bitcast.194), calls=%async_computation.3 | async-start | bytes 4194304 | tf_op jit(solution)/shard_map/all_to_all | solution.py:225
  214.4 15.7 %all-to-all-start.4 = ((bf16[8,32,1024]{2,1,0:T(8,128)(2,1)}), bf16[8,32,1024]{2,1,0:T(8,128)(2,1)}, u32[]{:S(2)}, u32[]{:S(2)}) async-start(bf16[8,32,1024]{2,1,0:T(8,128)(2,1)} %shard_map.106), calls=%async_computation.4 | async-start | bytes 1048576 | tf_op jit(solution)/shard_map/all_to_all | solution.py:245
  (28 other events, 342.7 us)

commit v3 on v2

--- a/solution.py
+++ b/solution.py
@@ -171,14 +171,16 @@
     mine = lax.dynamic_index_in_dim(by_core, core, 1, keepdims=False).reshape(-1, width)
     other = swap(lax.dynamic_index_in_dim(by_core, 1 - core, 1, keepdims=False), "c").reshape(-1, width)
     home_rows = jnp.concatenate(unrelated([mine, other], core), axis=1)
-    resident = got.transpose(1, 0, 2).reshape(quarter, wide).astype(F32)
-    squares = sum_over_x(jnp.sum(resident * resident, axis=1))
-    inverse = lax.rsqrt(squares / model + EPS)[:, None]
-    gain = lax.dynamic_slice_in_dim(attn_gain, x_pos * wide, wide).astype(F32)
-    normed = (resident * inverse * gain).astype(BF16)
-    z_pos = lax.axis_index("zl")
-    normed = jnp.concatenate(unrelated([normed[:, :rows], normed[:, rows:]], z_pos), axis=1)
-    normed = lax.ppermute(normed, WIDE, SPREAD)
+    resident = got.transpose(1, 0, 2).reshape(quarter, wide)
+    squares = sum_over_x(jnp.sum(jnp.square(resident.astype(F32)), axis=1))
+    inverse = lax.rsqrt(squares / model + EPS)
+    z_pos, plane = lax.axis_index("zl"), lax.axis_index(("yh", "zh"))
+    raw = jnp.concatenate(unrelated([resident[:, :rows], resident[:, rows:]], z_pos), axis=1)
+    raw = lax.ppermute(raw, WIDE, SPREAD)
+    inverse = lax.ppermute(inverse, WIDE, SPREAD)[:, None]
+    gain = lax.dynamic_slice_in_dim(attn_gain, plane * wide, wide).astype(F32)
+    gain = jnp.concatenate(unrelated([gain[:rows], gain[rows:]], z_pos))
+    normed = (raw.astype(F32) * inverse * gain).astype(BF16)
     slots = [normed] + [lax.ppermute(normed, "x", xor_pairs(k)) for k in (1, 2, 3)]
 
     order = lax.axis_index("x") ^ lax.axis_index(("yh", "zh"))

time: 261 us -> 265 us (1.015)
  starting transfers between devices: 86.7 us -> 94.5 us
  waiting for transfers between devices: 130 us -> 127 us
    ppermute x20, waiting for transfers between devices: 23.2 us -> 12.5 us  [swap(): return lax.ppermute(v, axis, FLIP)]
    all_to_all x1, waiting for transfers between devices: 1.14 us -> 11.2 us  [local(): got = lax.all_to_all(sent, PAIR, 0, 0, tiled=True)]
    ppermute x3, starting transfers between devices: 18.6 us -> 23.3 us  [local(): lax.ppermute(normed, 'x', xor_pairs(k))]
    all_to_all x2, starting transfers between devices: 10 us -> 13.4 us  [local(): arrived.append(lax.all_to_all(partial, WIDE, 0, 0, tiled=True))]
  transfers between devices with their start and end apart: 37 -> 38, of which waited for: 19 -> 18; matrix products, arithmetic and copies ran while one was open for 7% -> 6% of each run, Pallas kernels for 4% -> 4%
where the time goes in v3:
time: 265 us; the launch traced here: 264 us
  waiting for transfers between devices  127 us (48%)
  starting transfers between devices  94.5 us (36%)
  Pallas kernels  16 us (6%)
  local copies, waits for them, and re-layouts  10.3 us (4%)
  matrix products  8.73 us (3%)
  other arithmetic  6.19 us (2%)
    all_to_all x2, waiting for transfers between devices, local(): arrived.append(lax.all_to_all(partial, WIDE, 0, 0, tiled=True))  53.2 us
    ppermute x20, starting transfers between devices, swap(): return lax.ppermute(v, axis, FLIP)  25.9 us
    ppermute x3, starting transfers between devices, local(): lax.ppermute(normed, 'x', xor_pairs(k))  23.3 us
    all_to_all x1, waiting for transfers between devices, local(): lax.all_to_all(context, ACROSS, 0, 0, tiled=True).reshape(tokens, 2 * wide)  19.4 us
    pallas_call x3, Pallas kernels, matmul_kernel(): pl.pallas_call(body, out_shape=jax.ShapeDtypeStruct(out_shape, BF16), in_...  16 us
    all_to_all x2, starting transfers between devices, local(): arrived.append(lax.all_to_all(partial, WIDE, 0, 0, tiled=True))  13.4 us
    ppermute x3, waiting for transfers between devices, local(): lax.ppermute(normed, 'x', xor_pairs(k))  13.2 us
    ppermute x20, waiting for transfers between devices, swap(): return lax.ppermute(v, axis, FLIP)  12.5 us
  transfers between devices with their start and end apart: 38, of which 18 were waited for; matrix products, arithmetic and copies ran while one was open for 6% of the time, Pallas kernels for 4%

profile of v3, /device:TPU:1, one launch (start us, length us, event | category | flops | bytes accessed | tf_op | source)
XLA Modules:
  0.0 264.1 jit_solution(17802891988637371029)
XLA Ops:
  6.6 4.6 %all-to-all-start = ((bf16[4,64,512]{2,1,0:T(8,128)(2,1)}), bf16[4,64,512]{2,1,0:T(8,128)(2,1)S(1)}, u32[]{:S(2)}, u32[]{:S(2)}) async-start(bf16[4,64,512]{2,1,0:T(8,128)(2,1)} %bitcast.5), calls=%async_computation | async-start | bytes 524288 | tf_op jit(solution)/shard_map/all_to_all | solution.py:168
  12.0 11.2 %all-to-all-done = bf16[4,64,512]{2,1,0:T(8,128)(2,1)S(1)} async-done(((bf16[4,64,512]{2,1,0:T(8,128)(2,1)}), bf16[4,64,512]{2,1,0:T(8,128)(2,1)S(1)}, u32[]{:S(2)}, u32[]{:S(2)}) %all-to-all-start) | async-done | bytes 262176 | tf_op jit(solution)/shard_map/all_to_all | solution.py:168
  35.2 6.4 %collective-permute-done.8.refs_4_ = bf16[512,640]{1,0:T(8,128)(2,1)} collective-permute-done((bf16[512,640]{1,0:T(8,128)(2,1)S(1)}, bf16[512,640]{1,0:T(8,128)(2,1)}, u32[]{:S(2)}, u32[]{:S(2)}) %collective-permute-start.8) | collective-permute-done | bytes 655392 | tf_op jit(solution)/shard_map/ppermute | solution.py:58
  41.6 3.8 %collective-permute-start.5 = (bf16[64,2048]{1,0:T(8,128)(2,1)S(1)}, bf16[64,2048]{1,0:T(8,128)(2,1)S(1)}, u32[]{:S(2)}, u32[]{:S(2)}) collective-permute-start(bf16[64,2048]{1,0:T(8,128)(2,1)S(1)} %multiply_convert_fusion.1.refs_0_), channel_id=1, source_target_pairs={{0,4},{4,0},{8,12},{12,8},{1,5},{5,1},{9,13},{13,9},{2,6},{6,2},{1... | collective-permute-start | bytes 786440 | tf_op jit(solution)/shard_map/ppermute | solution.py:184
  51.2 14.8 %collective-permute-start.6 = (bf16[64,2048]{1,0:T(8,128)(2,1)S(1)}, bf16[64,2048]{1,0:T(8,128)(2,1)S(1)}, u32[]{:S(2)}, u32[]{:S(2)}) collective-permute-start(bf16[64,2048]{1,0:T(8,128)(2,1)S(1)} %multiply_convert_fusion.1.refs_0_), channel_id=1, source_target_pairs={{0,8},{4,12},{8,0},{12,4},{1,9},{5,13},{9,1},{13,5},{2,10},{6,14},... | collective-permute-start | bytes 786440 | tf_op jit(solution)/shard_map/ppermute | solution.py:184
  66.1 6.3 %collective-permute-done.6.refs_2_ = bf16[64,2048]{1,0:T(8,128)(2,1)S(1)} collective-permute-done((bf16[64,2048]{1,0:T(8,128)(2,1)S(1)}, bf16[64,2048]{1,0:T(8,128)(2,1)S(1)}, u32[]{:S(2)}, u32[]{:S(2)}) %collective-permute-start.6) | collective-permute-done | bytes 262176 | tf_op jit(solution)/shard_map/ppermute | solution.py:184
  72.3 4.6 %collective-permute-start.7 = (bf16[64,2048]{1,0:T(8,128)(2,1)S(1)}, bf16[64,2048]{1,0:T(8,128)(2,1)S(1)}, u32[]{:S(2)}, u32[]{:S(2)}) collective-permute-start(bf16[64,2048]{1,0:T(8,128)(2,1)S(1)} %multiply_convert_fusion.1.refs_0_), channel_id=1, source_target_pairs={{0,12},{4,8},{8,4},{12,0},{1,13},{5,9},{9,5},{13,1},{2,14},{6,10},... | collective-permute-start | bytes 786440 | tf_op jit(solution)/shard_map/ppermute | solution.py:184
  76.9 5.4 %collective-permute-done.7.refs_3_ = bf16[64,2048]{1,0:T(8,128)(2,1)S(1)} collective-permute-done((bf16[64,2048]{1,0:T(8,128)(2,1)S(1)}, bf16[64,2048]{1,0:T(8,128)(2,1)S(1)}, u32[]{:S(2)}, u32[]{:S(2)}) %collective-permute-start.7) | collective-permute-done | bytes 262176 | tf_op jit(solution)/shard_map/ppermute | solution.py:184
  85.7 5.3 %shard_map.105 = bf16[256,1280]{1,0:T(8,128)(2,1)} custom-call(s32[1]{0:T(128)} %bitcast.2.scalar_ref, bf16[64,2048]{1,0:T(8,128)(2,1)S(1)} %multiply_convert_fusion.1.refs_0_, bf16[64,2048]{1,0:T(8,128)(2,1)S(1)} %collective-permute-done.5.refs_1_, bf16[64,2048]{1,0:T(8,128)(2,1)S(1)} %collective-permute-done.6.refs_2_, ...), custom_call_target="tpu_custom_call" | custom-call | flops 1342177280 | bytes 5242880 | tf_op jit(solution)/shard_map/pallas_call | solution.py:122
  91.0 9.7 %all-to-all-start.2 = ((bf16[16,16,1280]{2,1,0:T(8,128)(2,1)}), bf16[16,16,1280]{2,1,0:T(8,128)(2,1)S(1)}, u32[]{:S(2)}, u32[]{:S(2)}) async-start(bf16[16,16,1280]{2,1,0:T(8,128)(2,1)} %bitcast.9), calls=%async_computation.2 | async-start | bytes 1310720 | tf_op jit(solution)/shard_map/all_to_all | solution.py:206
  104.9 5.1 %shard_map.104 = bf16[256,1280]{1,0:T(8,128)(2,1)} custom-call(s32[1]{0:T(128)} %bitcast.2.scalar_ref, bf16[64,2048]{1,0:T(8,128)(2,1)S(1)} %multiply_convert_fusion.1.refs_0_, bf16[64,2048]{1,0:T(8,128)(2,1)S(1)} %collective-permute-done.5.refs_1_, bf16[64,2048]{1,0:T(8,128)(2,1)S(1)} %collective-permute-done.6.refs_2_, ...), custom_call_target="tpu_custom_call" | custom-call | flops 1342177280 | bytes 5242880 | tf_op jit(solution)/shard_map/pallas_call | solution.py:122
  110.0 5.4 %all-to-all-done.2 = bf16[16,16,1280]{2,1,0:T(8,128)(2,1)S(1)} async-done(((bf16[16,16,1280]{2,1,0:T(8,128)(2,1)}), bf16[16,16,1280]{2,1,0:T(8,128)(2,1)S(1)}, u32[]{:S(2)}, u32[]{:S(2)}) %all-to-all-start.2) | async-done | bytes 655392 | tf_op jit(solution)/shard_map/all_to_all | solution.py:206
  115.4 3.8 %all-to-all-start.1 = ((bf16[16,16,1280]{2,1,0:T(8,128)(2,1)}), bf16[16,16,1280]{2,1,0:T(8,128)(2,1)S(1)}, u32[]{:S(2)}, u32[]{:S(2)}) async-start(bf16[16,16,1280]{2,1,0:T(8,128)(2,1)} %bitcast.7), calls=%async_computation.1 | async-start | bytes 1310720 | tf_op jit(solution)/shard_map/all_to_all | solution.py:206
  119.6 47.8 %all-to-all-done.1 = bf16[16,16,1280]{2,1,0:T(8,128)(2,1)S(1)} async-done(((bf16[16,16,1280]{2,1,0:T(8,128)(2,1)}), bf16[16,16,1280]{2,1,0:T(8,128)(2,1)S(1)}, u32[]{:S(2)}, u32[]{:S(2)}) %all-to-all-start.1) | async-done | bytes 655392 | tf_op jit(solution)/shard_map/all_to_all | solution.py:206
  169.3 6.6 %fusion.31 = (f32[16,8,8]{2,1,0:T(8,128)S(1)}, f32[16,8,8,192]{3,2,1,0:T(8,128)S(1)}) fusion(bf16[16,8,192,128]{3,2,1,0:T(8,128)(2,1)} %param.15, bf16[16,8,8,64]{3,2,1,0:T(8,128)(2,1)S(1)} %get-tuple-element.7, bf16[16,8,8,64]{3,2,1,0:T(8,128)(2,1)S(1)} %get-tuple-element.6, pred[16,192]{1,0:T(8,128)(4,1)S(1)} %iota_compare_fusion), kind=kOutput, calls=%fused_computation.140 | convolution fusion | flops 51444736 | bytes 7347200 | tf_op jit(solution)/shard_map/nkgd,nkld->nkgl/dot_general | solution.py:31
  180.2 3.7 %all-to-all-start.3 = ((bf16[16,16,4096]{2,1,0:T(8,128)(2,1)}), bf16[16,16,4096]{2,1,0:T(8,128)(2,1)S(1)}, u32[]{:S(2)}, u32[]{:S(2)}) async-start(bf16[16,16,4096]{2,1,0:T(8,128)(2,1)} %bitcast.194), calls=%async_computation.3 | async-start | bytes 4194304 | tf_op jit(solution)/shard_map/all_to_all | solution.py:227
  192.7 19.4 %all-to-all-done.3 = bf16[16,16,4096]{2,1,0:T(8,128)(2,1)S(1)} async-done(((bf16[16,16,4096]{2,1,0:T(8,128)(2,1)}), bf16[16,16,4096]{2,1,0:T(8,128)(2,1)S(1)}, u32[]{:S(2)}, u32[]{:S(2)}) %all-to-all-start.3) | async-done | bytes 2097184 | tf_op jit(solution)/shard_map/all_to_all | solution.py:227
  212.1 5.6 %shard_map.106 = bf16[8,32,1024]{2,1,0:T(8,128)(2,1)} custom-call(s32[2]{0:T(128)S(1)} %pad_add_fusion.scalar_ref, bf16[256,4096]{1,0:T(8,128)(2,1)S(1)} %bitcast.193, bf16[512,1024]{1,0:T(8,128)(2,1)} %refs_1_.1, bf16[512,1024]{1,0:T(8,128)(2,1)} %copy-done.4, bf16[512,1024]{1,0:T(8,128)(2,1)} %collective-permute-done.23.refs_3_, ...), custom_call_target="tpu_custom_call" | custom-call | flops 2147483648 | bytes 8388608 | tf_op jit(solution)/shard_map/pallas_call | solution.py:122
  217.7 7.3 %all-to-all-start.4 = ((bf16[8,32,1024]{2,1,0:T(8,128)(2,1)}), bf16[8,32,1024]{2,1,0:T(8,128)(2,1)}, u32[]{:S(2)}, u32[]{:S(2)}) async-start(bf16[8,32,1024]{2,1,0:T(8,128)(2,1)} %shard_map.106), calls=%async_computation.4 | async-start | bytes 1048576 | tf_op jit(solution)/shard_map/all_to_all | solution.py:247
  225.0 9.3 %all-to-all-done.4 = bf16[8,32,1024]{2,1,0:T(8,128)(2,1)} async-done(((bf16[8,32,1024]{2,1,0:T(8,128)(2,1)}), bf16[8,32,1024]{2,1,0:T(8,128)(2,1)}, u32[]{:S(2)}, u32[]{:S(2)}) %all-to-all-start.4) | async-done | bytes 524320 | tf_op jit(solution)/shard_map/all_to_all | solution.py:247
  234.3 3.5 %all-to-all-start.5 = ((bf16[8,32,1024]{2,1,0:T(8,128)(2,1)}), bf16[8,32,1024]{2,1,0:T(8,128)(2,1)S(1)}, u32[]{:S(2)}, u32[]{:S(2)}) async-start(bf16[8,32,1024]{2,1,0:T(8,128)(2,1)} %all-to-all-done.4), calls=%async_computation.5 | async-start | bytes 1048576 | tf_op jit(solution)/shard_map/all_to_all | solution.py:248
  245.7 3.5 %all-to-all-start.6 = ((f32[8,1,128]{2,1,0:T(1,128)}), f32[8,1,128]{2,1,0:T(1,128)S(1)}, u32[]{:S(2)}, u32[]{:S(2)}) async-start(f32[8,1,128]{2,1,0:T(1,128)} %broadcast_in_dim.25), calls=%async_computation.6 | async-start | bytes 8192 | tf_op jit(solution)/shard_map/all_to_all | solution.py:252
  250.2 3.7 %all-to-all-done.6 = f32[8,1,128]{2,1,0:T(1,128)S(1)} async-done(((f32[8,1,128]{2,1,0:T(1,128)}), f32[8,1,128]{2,1,0:T(1,128)S(1)}, u32[]{:S(2)}, u32[]{:S(2)}) %all-to-all-start.6) | async-done | bytes 4128 | tf_op jit(solution)/shard_map/all_to_all | solution.py:252
  256.3 5.0 %collective-permute-start.30 = (bf16[2,128,512]{2,1,0:T(8,128)(2,1)S(1)}, bf16[2,128,512]{2,1,0:T(8,128)(2,1)S(1)}, u32[]{:S(2)}, u32[]{:S(2)}) collective-permute-start(bf16[2,128,512]{2,1,0:T(8,128)(2,1)S(1)} %bitcast.211), channel_id=1, source_target_pairs={{0,1},{1,0},{2,3},{3,2},{4,5},{5,4},{6,7},{7,6},{8,9},{9,8},{10,11... | collective-permute-start | bytes 786440 | tf_op jit(solution)/shard_map/ppermute | solution.py:58
  (181 shorter events, 60.9 us)
Async XLA Ops:
  2.1 32.9 %collective-permute-start.12 = (bf16[512,640]{1,0:T(8,128)(2,1)S(1)}, bf16[512,640]{1,0:T(8,128)(2,1)S(1)}, u32[]{:S(2)}, u32[]{:S(2)}) collective-permute-start(bf16[512,640]{1,0:T(8,128)(2,1)S(1)} %pad_maximum_fusion.1.refs_4_), channel_id=1, source_target_pairs={{0,16},{16,0},{1,17},{17,1},{2,18},{18,2},{3,19},{19,3},{4,20},{20... | collective-permute-start | bytes 1966088 | tf_op jit(solution)/shard_map/ppermute | solution.py:58
  4.6 40.8 %collective-permute-start.10 = (bf16[512,640]{1,0:T(8,128)(2,1)S(1)}, bf16[512,640]{1,0:T(8,128)(2,1)}, u32[]{:S(2)}, u32[]{:S(2)}) collective-permute-start(bf16[512,640]{1,0:T(8,128)(2,1)S(1)} %pad_maximum_fusion.1.refs_4_), channel_id=1, source_target_pairs={{0,2},{2,0},{1,3},{3,1},{4,6},{6,4},{5,7},{7,5},{8,10},{10,8},{9,1... | collective-permute-start | bytes 1966088 | tf_op jit(solution)/shard_map/ppermute | solution.py:58
  6.6 16.5 %all-to-all-start = ((bf16[4,64,512]{2,1,0:T(8,128)(2,1)}), bf16[4,64,512]{2,1,0:T(8,128)(2,1)S(1)}, u32[]{:S(2)}, u32[]{:S(2)}) async-start(bf16[4,64,512]{2,1,0:T(8,128)(2,1)} %bitcast.5), calls=%async_computation | async-start | bytes 524288 | tf_op jit(solution)/shard_map/all_to_all | solution.py:168
  27.4 14.2 %collective-permute-start.8 = (bf16[512,640]{1,0:T(8,128)(2,1)S(1)}, bf16[512,640]{1,0:T(8,128)(2,1)}, u32[]{:S(2)}, u32[]{:S(2)}) collective-permute-start(bf16[512,640]{1,0:T(8,128)(2,1)S(1)} %pad_maximum_fusion.refs_6_), channel_id=1, source_target_pairs={{0,2},{2,0},{1,3},{3,1},{4,6},{6,4},{5,7},{7,5},{8,10},{10,8},{9,1... | collective-permute-start | bytes 1966088 | tf_op jit(solution)/shard_map/ppermute | solution.py:58
  31.4 15.3 %collective-permute-start.20 = (bf16[512,640]{1,0:T(8,128)(2,1)S(1)}, bf16[512,640]{1,0:T(8,128)(2,1)}, u32[]{:S(2)}, u32[]{:S(2)}) collective-permute-start(bf16[512,640]{1,0:T(8,128)(2,1)S(1)} %pad_maximum_fusion.refs_6_), channel_id=1, source_target_pairs={{0,16},{16,0},{1,17},{17,1},{2,18},{18,2},{3,19},{19,3},{4,20},{20... | collective-permute-start | bytes 1966088 | tf_op jit(solution)/shard_map/ppermute | solution.py:58
  31.6 16.8 %collective-permute-start.17 = (bf16[512,640]{1,0:T(8,128)(2,1)S(1)}, bf16[512,640]{1,0:T(8,128)(2,1)S(1)}, u32[]{:S(2)}, u32[]{:S(2)}) collective-permute-start(bf16[512,640]{1,0:T(8,128)(2,1)S(1)} %pad_maximum_fusion.1.refs_4_), channel_id=1, source_target_pairs={{0,1},{1,0},{2,3},{3,2},{4,5},{5,4},{6,7},{7,6},{8,9},{9,8},{10,11... | collective-permute-start | bytes 1966088 | tf_op jit(solution)/shard_map/ppermute | solution.py:58
  35.0 14.7 %collective-permute-start.18 = (bf16[512,640]{1,0:T(8,128)(2,1)S(1)}, bf16[512,640]{1,0:T(8,128)(2,1)S(1)}, u32[]{:S(2)}, u32[]{:S(2)}) collective-permute-start(bf16[512,640]{1,0:T(8,128)(2,1)S(1)} %pad_maximum_fusion.refs_6_), channel_id=1, source_target_pairs={{0,1},{1,0},{2,3},{3,2},{4,5},{5,4},{6,7},{7,6},{8,9},{9,8},{10,11... | collective-permute-start | bytes 1966088 | tf_op jit(solution)/shard_map/ppermute | solution.py:58
  45.5 38.8 %collective-permute-start.13 = (bf16[512,640]{1,0:T(8,128)(2,1)S(1)}, bf16[512,640]{1,0:T(8,128)(2,1)}, u32[]{:S(2)}, u32[]{:S(2)}) collective-permute-start(bf16[512,640]{1,0:T(8,128)(2,1)S(1)} %collective-permute-done.12.refs_8_), channel_id=1, source_target_pairs={{0,2},{2,0},{1,3},{3,1},{4,6},{6,4},{5,7},{7,5},{8,10},{10,8},{9,1... | collective-permute-start | bytes 1966088 | tf_op jit(solution)/shard_map/ppermute | solution.py:58
  46.8 37.5 %collective-permute-start.15 = (bf16[512,640]{1,0:T(8,128)(2,1)}, bf16[512,640]{1,0:T(8,128)(2,1)}, u32[]{:S(2)}, u32[]{:S(2)}) collective-permute-start(bf16[512,640]{1,0:T(8,128)(2,1)} %collective-permute-done.8.refs_4_), channel_id=1, source_target_pairs={{0,16},{16,0},{1,17},{17,1},{2,18},{18,2},{3,19},{19,3},{4,20},{20... | collective-permute-start | bytes 1966088 | tf_op jit(solution)/shard_map/ppermute | solution.py:58
  48.4 36.3 %collective-permute-start.19 = (bf16[512,640]{1,0:T(8,128)(2,1)S(1)}, bf16[512,640]{1,0:T(8,128)(2,1)S(1)}, u32[]{:S(2)}, u32[]{:S(2)}) collective-permute-start(bf16[512,640]{1,0:T(8,128)(2,1)S(1)} %collective-permute-done.12.refs_8_), channel_id=1, source_target_pairs={{0,1},{1,0},{2,3},{3,2},{4,5},{5,4},{6,7},{7,6},{8,9},{9,8},{10,11... | collective-permute-start | bytes 1966088 | tf_op jit(solution)/shard_map/ppermute | solution.py:58
  49.7 36.0 %collective-permute-start.21 = (bf16[512,640]{1,0:T(8,128)(2,1)}, bf16[512,640]{1,0:T(8,128)(2,1)}, u32[]{:S(2)}, u32[]{:S(2)}) collective-permute-start(bf16[512,640]{1,0:T(8,128)(2,1)} %collective-permute-done.20.refs_10_), channel_id=1, source_target_pairs={{0,1},{1,0},{2,3},{3,2},{4,5},{5,4},{6,7},{7,6},{8,9},{9,8},{10,11... | collective-permute-start | bytes 1966088 | tf_op jit(solution)/shard_map/ppermute | solution.py:58
  51.2 21.1 %collective-permute-start.6 = (bf16[64,2048]{1,0:T(8,128)(2,1)S(1)}, bf16[64,2048]{1,0:T(8,128)(2,1)S(1)}, u32[]{:S(2)}, u32[]{:S(2)}) collective-permute-start(bf16[64,2048]{1,0:T(8,128)(2,1)S(1)} %multiply_convert_fusion.1.refs_0_), channel_id=1, source_target_pairs={{0,8},{4,12},{8,0},{12,4},{1,9},{5,13},{9,1},{13,5},{2,10},{6,14},... | collective-permute-start | bytes 786440 | tf_op jit(solution)/shard_map/ppermute | solution.py:184
  82.4 19.9 %collective-permute-start.9 = (bf16[512,640]{1,0:T(8,128)(2,1)}, bf16[512,640]{1,0:T(8,128)(2,1)}, u32[]{:S(2)}, u32[]{:S(2)}) collective-permute-start(bf16[512,640]{1,0:T(8,128)(2,1)} %collective-permute-done.8.refs_4_), channel_id=1, source_target_pairs={{0,1},{1,0},{2,3},{3,2},{4,5},{5,4},{6,7},{7,6},{8,9},{9,8},{10,11... | collective-permute-start | bytes 1966088 | tf_op jit(solution)/shard_map/ppermute | solution.py:58
  84.2 20.0 %collective-permute-start.11 = (bf16[512,640]{1,0:T(8,128)(2,1)}, bf16[512,640]{1,0:T(8,128)(2,1)}, u32[]{:S(2)}, u32[]{:S(2)}) collective-permute-start(bf16[512,640]{1,0:T(8,128)(2,1)} %collective-permute-done.10.refs_6_), channel_id=1, source_target_pairs={{0,1},{1,0},{2,3},{3,2},{4,5},{5,4},{6,7},{7,6},{8,9},{9,8},{10,11... | collective-permute-start | bytes 1966088 | tf_op jit(solution)/shard_map/ppermute | solution.py:58
  84.2 20.7 %collective-permute-start.14 = (bf16[512,640]{1,0:T(8,128)(2,1)}, bf16[512,640]{1,0:T(8,128)(2,1)}, u32[]{:S(2)}, u32[]{:S(2)}) collective-permute-start(bf16[512,640]{1,0:T(8,128)(2,1)} %collective-permute-done.13.refs_8_), channel_id=1, source_target_pairs={{0,1},{1,0},{2,3},{3,2},{4,5},{5,4},{6,7},{7,6},{8,9},{9,8},{10,11... | collective-permute-start | bytes 1966088 | tf_op jit(solution)/shard_map/ppermute | solution.py:58
  85.6 19.3 %collective-permute-start.16 = (bf16[512,640]{1,0:T(8,128)(2,1)}, bf16[512,640]{1,0:T(8,128)(2,1)}, u32[]{:S(2)}, u32[]{:S(2)}) collective-permute-start(bf16[512,640]{1,0:T(8,128)(2,1)} %collective-permute-done.15.refs_10_), channel_id=1, source_target_pairs={{0,1},{1,0},{2,3},{3,2},{4,5},{5,4},{6,7},{7,6},{8,9},{9,8},{10,11... | collective-permute-start | bytes 1966088 | tf_op jit(solution)/shard_map/ppermute | solution.py:58
  91.0 24.5 %all-to-all-start.2 = ((bf16[16,16,1280]{2,1,0:T(8,128)(2,1)}), bf16[16,16,1280]{2,1,0:T(8,128)(2,1)S(1)}, u32[]{:S(2)}, u32[]{:S(2)}) async-start(bf16[16,16,1280]{2,1,0:T(8,128)(2,1)} %bitcast.9), calls=%async_computation.2 | async-start | bytes 1310720 | tf_op jit(solution)/shard_map/all_to_all | solution.py:206
  100.7 85.1 %collective-permute-start.23 = (bf16[512,1024]{1,0:T(8,128)(2,1)S(1)}, bf16[512,1024]{1,0:T(8,128)(2,1)}, u32[]{:S(2)}, u32[]{:S(2)}) collective-permute-start(bf16[512,1024]{1,0:T(8,128)(2,1)S(1)} %copy-done.3), channel_id=1, source_target_pairs={{0,4},{4,0},{8,12},{12,8},{1,5},{5,1},{9,13},{13,9},{2,6},{6,2},{1... | collective-permute-start | bytes 3145736 | tf_op jit(solution)/shard_map/ppermute | solution.py:81
  102.3 83.6 %collective-permute-start.25 = (bf16[512,1024]{1,0:T(8,128)(2,1)S(1)}, bf16[512,1024]{1,0:T(8,128)(2,1)}, u32[]{:S(2)}, u32[]{:S(2)}) collective-permute-start(bf16[512,1024]{1,0:T(8,128)(2,1)S(1)} %copy-done.3), channel_id=1, source_target_pairs={{0,12},{4,8},{8,4},{12,0},{1,13},{5,9},{9,5},{13,1},{2,14},{6,10},... | collective-permute-start | bytes 3145736 | tf_op jit(solution)/shard_map/ppermute | solution.py:81
  104.2 82.1 %collective-permute-start.27 = (bf16[512,1024]{1,0:T(8,128)(2,1)S(1)}, bf16[512,1024]{1,0:T(8,128)(2,1)}, u32[]{:S(2)}, u32[]{:S(2)}) collective-permute-start(bf16[512,1024]{1,0:T(8,128)(2,1)S(1)} %copy-done.3), channel_id=1, source_target_pairs={{0,8},{4,12},{8,0},{12,4},{1,9},{5,13},{9,1},{13,5},{2,10},{6,14},... | collective-permute-start | bytes 3145736 | tf_op jit(solution)/shard_map/ppermute | solution.py:82
  115.4 52.0 %all-to-all-start.1 = ((bf16[16,16,1280]{2,1,0:T(8,128)(2,1)}), bf16[16,16,1280]{2,1,0:T(8,128)(2,1)S(1)}, u32[]{:S(2)}, u32[]{:S(2)}) async-start(bf16[16,16,1280]{2,1,0:T(8,128)(2,1)} %bitcast.7), calls=%async_computation.1 | async-start | bytes 1310720 | tf_op jit(solution)/shard_map/all_to_all | solution.py:206
  180.2 32.0 %all-to-all-start.3 = ((bf16[16,16,4096]{2,1,0:T(8,128)(2,1)}), bf16[16,16,4096]{2,1,0:T(8,128)(2,1)S(1)}, u32[]{:S(2)}, u32[]{:S(2)}) async-start(bf16[16,16,4096]{2,1,0:T(8,128)(2,1)} %bitcast.194), calls=%async_computation.3 | async-start | bytes 4194304 | tf_op jit(solution)/shard_map/all_to_all | solution.py:227
  217.7 16.5 %all-to-all-start.4 = ((bf16[8,32,1024]{2,1,0:T(8,128)(2,1)}), bf16[8,32,1024]{2,1,0:T(8,128)(2,1)}, u32[]{:S(2)}, u32[]{:S(2)}) async-start(bf16[8,32,1024]{2,1,0:T(8,128)(2,1)} %shard_map.106), calls=%async_computation.4 | async-start | bytes 1048576 | tf_op jit(solution)/shard_map/all_to_all | solution.py:247
  234.3 10.5 %all-to-all-start.5 = ((bf16[8,32,1024]{2,1,0:T(8,128)(2,1)}), bf16[8,32,1024]{2,1,0:T(8,128)(2,1)S(1)}, u32[]{:S(2)}, u32[]{:S(2)}) async-start(bf16[8,32,1024]{2,1,0:T(8,128)(2,1)} %all-to-all-done.4), calls=%async_computation.5 | async-start | bytes 1048576 | tf_op jit(solution)/shard_map/all_to_all | solution.py:248
  (29 other events, 357.2 us)
